TPU v7x, 8 devices: a whole 2x2x1 slice. The times are simulated.
8 devices in a mesh: data: 1 (over z), expert: 8 (over y, x, core).
Axes of the slice: x: 2, y: 2, z: 1, core: 2. Of those that a mesh axis runs over, the one named last changes fastest.
Arguments:
- token_rows: bfloat16 [16384, 512], P(('data', 'expert'))
- expert_ids: int32 [16384, 2], P(('data', 'expert'))
- gate_weights: float32 [16384, 2], P(('data', 'expert'))
- w_in: bfloat16 [512, 512, 1024], P('expert')
- w_out: bfloat16 [512, 1024, 512], P('expert')
Outputs:
- output: bfloat16 [16384, 512], P(('data', 'expert'))
All inputs are finite; a program needn't handle non-finite values.
Results may differ from a plain program's by a relative error of at most 0.001.
Values are sent between devices in bfloat16 or wider.
A program may use at most 1 GiB of HBM per device.

v0:
```python
import jax
import jax.numpy as jnp
from jax import lax
from jax.sharding import PartitionSpec as P


def route_local(expert_ids, experts):
    ids_t = expert_ids.T
    onehot = (ids_t[:, :, None] == jnp.arange(experts, dtype=jnp.int32)).astype(jnp.int32)
    running = jnp.cumsum(onehot, axis=1)
    counts = running[:, -1, :]
    rank_local = jnp.sum(onehot * running, axis=2) - 1
    return ids_t, counts, rank_local


def solution(mesh):
    groups = mesh.shape["expert"]
    row_spec = P(("data", "expert"), None)
    weight_spec = P("expert", None, None)

    def device_step(token_rows, expert_ids, gate_weights, w_in, w_out):
        tokens, top_k = expert_ids.shape
        local_experts, model_dim = w_in.shape[0], w_in.shape[1]
        experts = local_experts * groups
        mean_load = tokens * top_k // experts
        send_cap = 7 * mean_load // 4
        capacity = groups * mean_load
        rows_total = experts * send_cap
        ids_t, counts, rank_local = route_local(expert_ids, experts)
        inclusive = counts
        shift = 1
        while shift < groups:
            pairs_list = [(source, source + shift) for source in range(groups - shift)]
            inclusive = inclusive + lax.ppermute(inclusive, "expert", pairs_list)
            shift = shift * 2
        before = inclusive - counts
        totals = lax.psum(counts, "expert")
        prior = jnp.cumsum(totals, axis=0) - totals
        within = jnp.cumsum(counts, axis=0) - counts
        slot = jnp.take_along_axis(prior + before, ids_t, axis=1) + rank_local
        keep = slot < capacity
        target = ids_t * send_cap + jnp.take_along_axis(within, ids_t, axis=1) + rank_local
        token_ids = jnp.broadcast_to(jnp.arange(tokens, dtype=jnp.int32), (top_k, tokens))
        source_row = jnp.full((rows_total,), tokens, jnp.int32).at[jnp.where(keep, target, rows_total).reshape(-1)].set(token_ids.reshape(-1), mode="drop")
        padded = jnp.concatenate([token_rows, jnp.zeros((1, model_dim), token_rows.dtype)], axis=0)
        outbound = jnp.take(padded, source_row, axis=0).reshape(experts, send_cap, model_dim)
        inbound = lax.all_to_all(outbound, "expert", 0, 0, tiled=True).reshape(groups, local_experts, send_cap, model_dim)
        pre_act = jnp.einsum("gesd,edf->gesf", inbound, w_in, preferred_element_type=jnp.float32)
        hidden = jax.nn.gelu(pre_act).astype(jnp.bfloat16)
        expert_out = jnp.einsum("gesf,efd->gesd", hidden, w_out, preferred_element_type=jnp.float32).astype(jnp.bfloat16)
        returned = lax.all_to_all(expert_out.reshape(experts, send_cap, model_dim), "expert", 0, 0, tiled=True).reshape(rows_total, model_dim)
        picked = jnp.take(returned, target, axis=0)
        weight = jnp.where(keep, gate_weights.T, 0.0)
        mixed = jnp.sum(weight[:, :, None] * picked.astype(jnp.float32), axis=0)
        return (token_rows.astype(jnp.float32) + mixed).astype(jnp.bfloat16)

    return jax.shard_map(device_step, mesh=mesh, in_specs=(row_spec, row_spec, row_spec, weight_spec, weight_spec), out_specs=row_spec, check_vma=False)
```

profile of v0, /device:TPU:1, one launch (start us, length us, event | category | flops | bytes accessed | tf_op | source)
XLA Modules:
  0.0 483.5 jit_solution(7799636063569528563)
XLA Ops:
  0.0 0.7 copy.47
  0.7 0.1 copy.13
  0.8 1.0 fusion.26
  1.9 0.0 copy-start
  1.9 3.2 copy-done
  5.1 0.1 reduce-window.9
  5.2 4.5 broadcast_add_fusion
  9.6 0.0 copy-start.2
  9.7 4.9 %copy.14 = s32[2,512,16,128]{1,3,2,0:T(8,128)S(1)} copy(s32[2,512,16,128]{1,2,3,0:T(8,128)S(1)} %broadcast_add_fusion) | data formatting | bytes 16777216 | tf_op jit(solution)/shard_map/reduce_window_sum
  14.5 4.5 collective-permute-start
  19.1 0.0 copy-done.2
  19.1 2.2 select_reduce_fusion
  21.3 0.0 collective-permute-done
  21.3 3.1 collective-permute-start.1
  24.5 21.2 %psum.7 = s32[2,512]{1,0:T(2,128)S(1)} all-reduce(s32[2,512]{1,0:T(2,128)S(1)} %bitcast.99), channel_id=1, replica_groups=mesh['data'=1,'expert'=8] {'expert'}, use_global_device_ids=true, to_apply=%region_2.3 | all-reduce | flops 1024 | bytes 8192 | tf_op jit(solution)/shard_map/psum | solution.py:37
  45.7 1.7 concatenate.3
  47.4 34.9 %gather_fusion.3 = s32[4096]{0:T(1024)S(1)} fusion(s32[2,512]{1,0:T(2,128)S(1)} %get-tuple-element.12, s32[4096]{0:T(1024)S(1)} %bitcast.86), kind=kCustom, calls=%fused_computation.1.clone | custom fusion | bytes 65536 | tf_op jit(solution)/shard_map/jit(take_along_axis)/gather | solution.py:42
  82.3 0.0 collective-permute-done.1
  82.4 4.3 collective-permute-start.2
  86.7 0.1 compare_and_fusion.1
  86.8 0.7 collective-permute-done.2
  87.5 0.0 copy-start.3
  87.5 34.9 %gather_fusion.2 = s32[4096]{0:T(1024)S(1)} fusion(s32[2,512]{1,0:T(2,128)S(1)} %subtract_add_fusion, s32[4096]{0:T(1024)S(1)} %bitcast.87), kind=kCustom, calls=%fused_computation.clone | custom fusion | bytes 65536 | tf_op jit(solution)/shard_map/jit(take_along_axis)/gather | solution.py:40
  122.4 0.0 copy-done.3
  122.5 15.7 %scatter_custom_fusion = s32[7168]{0:T(1024)S(1)} fusion(s32[4096]{0:T(1024)S(1)} %bitcast.101, s32[4096]{0:T(1024)S(1)} %bitcast.100, s32[]{:T(128)} %constant.44.clone.1), kind=kCustom, calls=%fused_computation.53 | custom fusion | bytes 28676 | tf_op jit(solution)/shard_map/scatter | solution.py:44
  138.3 29.5 %gather_fusion = bf16[7168,512]{1,0:T(8,128)(2,1)} fusion(bf16[2049,512]{1,0:T(8,128)(2,1)S(1)} %concatenate.3, s32[7168]{0:T(1024)S(1)} %fusion.37), kind=kCustom, calls=%fused_computation.2 | custom fusion | bytes 14708736 | tf_op jit(solution)/shard_map/jit(_take)/gather | solution.py:46
  167.8 11.9 %gather.14 = bf16[512,14,512]{2,1,0:T(8,128)(2,1)} reshape(bf16[7168,512]{1,0:T(8,128)(2,1)} %gather_fusion) | data formatting | bytes 14680064 | tf_op jit(solution)/shard_map/jit(_take)/gather | solution.py:46
  179.7 0.3 broadcast_in_dim.50
  179.9 4.7 broadcast_select_fusion
  184.6 98.1 %all_to_all.10 = bf16[512,14,512]{2,1,0:T(8,128)(2,1)} all-to-all(bf16[512,14,512]{2,1,0:T(8,128)(2,1)S(1)} %broadcast_select_fusion), channel_id=1, replica_groups=mesh['data'=1,'expert'=8] {'expert'}, dimensions={0} | all-to-all | bytes 14680064 | tf_op jit(solution)/shard_map/all_to_all | solution.py:47
  282.7 51.2 %convert_bitcast_fusion = bf16[8,64,14,512]{3,2,0,1:T(8,128)(2,1)} fusion(bf16[64,1024,512]{2,1,0:T(8,128)(2,1)} %param.11, bf16[64,512,1024]{2,1,0:T(8,128)(2,1)} %param.10, bf16[8,64,14,512]{3,2,1,0:T(8,128)(2,1)} %bitcast.91), kind=kOutput, calls=%fused_computation.24 | convolution fusion | flops 15102115840 | bytes 148897792 | tf_op jit(solution)/shard_map/gesf,efd->gesd/dot_general | solution.py:50
  333.9 7.5 %copy.17 = bf16[8,64,14,512]{3,1,0,2:T(8,128)(2,1)S(1)} copy(bf16[8,64,14,512]{3,2,0,1:T(8,128)(2,1)} %convert_bitcast_fusion) | data formatting | bytes 14680064 | tf_op jit(solution)/shard_map/convert_element_type | solution.py:50
  341.4 7.6 %copy.18 = bf16[512,14,512]{2,1,0:T(8,128)(2,1)} copy(bf16[512,14,512]{2,0,1:T(8,128)(2,1)S(1)} %bitcast.89) | data formatting | bytes 14680064 | tf_op jit(solution)/shard_map/reshape | solution.py:51
  349.0 4.8 all-to-all-start.1
  353.8 90.0 %all-to-all-done.1 = bf16[512,14,512]{2,1,0:T(8,128)(2,1)} async-done(((bf16[512,14,512]{2,1,0:T(8,128)(2,1)}), bf16[512,14,512]{2,1,0:T(8,128)(2,1)}, u32[]{:S(2)}, u32[]{:S(2)}) %all-to-all-start.1) | async-done | bytes 7340064 | tf_op jit(solution)/shard_map/all_to_all | solution.py:51
  443.9 11.9 %reshape.86 = bf16[7168,512]{1,0:T(8,128)(2,1)} reshape(bf16[512,14,512]{2,1,0:T(8,128)(2,1)} %all-to-all-done.1) | data formatting | bytes 14680064 | tf_op jit(solution)/shard_map/reshape | solution.py:51
  455.8 21.4 %gather_fusion.1 = bf16[4096,512]{1,0:T(8,128)(2,1)} fusion(bf16[7168,512]{1,0:T(8,128)(2,1)} %reshape.86, s32[4096]{0:T(1024)S(1)} %broadcast_clamp_fusion), kind=kCustom, calls=%fused_computation.3 | custom fusion | bytes 8404992 | tf_op jit(solution)/shard_map/jit(_take)/gather | solution.py:52
  477.2 0.0 copy-start.1
  477.2 4.2 multiply_reduce_fusion
  481.4 0.0 copy-done.1
  481.4 2.1 add_convert_fusion
  (23 shorter events, 0.3 us)
Async XLA Ops:
  1.9 3.2 copy-start
  9.6 9.4 %copy-start.2 = (s32[2048,2]{0,1:T(2,128)S(1)}, s32[2048,2]{0,1:T(2,128)}, u32[]{:S(2)}) copy-start(s32[2048,2]{0,1:T(2,128)} %param.8) | copy-start | bytes 49156
  14.5 6.8 %collective-permute-start = (s32[2,512]{1,0:T(2,128)S(1)}, s32[2,512]{1,0:T(2,128)S(1)}, u32[]{:S(2)}, u32[]{:S(2)}) collective-permute-start(s32[2,512]{1,0:T(2,128)S(1)} %bitcast.97), channel_id=1, source_target_pairs={{0,1},{1,2},{2,3},{3,4},{4,5},{5,6},{6,7}} | collective-permute-start | bytes 12296 | tf_op jit(solution)/shard_map/ppermute | solution.py:34
  21.3 61.0 %collective-permute-start.1 = (s32[2,512]{1,0:T(2,128)S(1)}, s32[2,512]{1,0:T(2,128)S(1)}, u32[]{:S(2)}, u32[]{:S(2)}) collective-permute-start(s32[2,512]{1,0:T(2,128)S(1)} %get-tuple-element.13), channel_id=1, source_target_pairs={{0,2},{1,3},{2,4},{3,5},{4,6},{5,7}} | collective-permute-start | bytes 12296 | tf_op jit(solution)/shard_map/ppermute | solution.py:34
  82.4 5.1 %collective-permute-start.2 = (s32[2,512]{1,0:T(2,128)S(1)}, s32[2,512]{1,0:T(2,128)S(1)}, u32[]{:S(2)}, u32[]{:S(2)}) collective-permute-start(s32[2,512]{1,0:T(2,128)S(1)} %add.74), channel_id=1, source_target_pairs={{0,4},{1,5},{2,6},{3,7}} | collective-permute-start | bytes 12296 | tf_op jit(solution)/shard_map/ppermute | solution.py:34
  87.5 34.9 %copy-start.3 = (f32[2048,2]{0,1:T(2,128)S(1)}, f32[2048,2]{0,1:T(2,128)}, u32[]{:S(2)}) copy-start(f32[2048,2]{0,1:T(2,128)} %param.9) | copy-start | bytes 49156
  349.0 94.9 %all-to-all-start.1 = ((bf16[512,14,512]{2,1,0:T(8,128)(2,1)}), bf16[512,14,512]{2,1,0:T(8,128)(2,1)}, u32[]{:S(2)}, u32[]{:S(2)}) async-start(bf16[512,14,512]{2,1,0:T(8,128)(2,1)} %copy.18), calls=%async_computation.1 | async-start | bytes 16777216 | tf_op jit(solution)/shard_map/all_to_all | solution.py:51
  477.2 4.2 copy-start.1
where the time goes:
time: 489 us; the launch traced here: 484 us
  local copies, waits for them, and re-layouts  186 us (38%)
  blocking collectives  119 us (24%)
  waiting for transfers between devices  90.7 us (19%)
  matrix products  51.2 us (10%)
  other arithmetic  19 us (4%)
  starting transfers between devices  16.8 us (3%)
    all_to_all x1, blocking collectives, device_step(): lax.all_to_all(outbound, 'expert', 0, 0, tiled=True)  98.1 us
    all_to_all x1, waiting for transfers between devices, device_step(): lax.all_to_all(expert_out.reshape(experts, send_cap, model_dim), 'expert'...  90 us
    dot_general x1, matrix products, device_step(): jnp.einsum('gesf,efd->gesd', hidden, w_out, preferred_element_type=jnp.fl...  51.2 us
    gather x2, local copies, waits for them, and re-layouts, device_step(): jnp.take(padded, source_row, axis=0).reshape(experts, send_cap, model_dim)  41.4 us
    gather x2, local copies, waits for them, and re-layouts, device_step(): jnp.take_along_axis(within, ids_t, axis=1)  34.9 us
    gather x2, local copies, waits for them, and re-layouts, device_step(): slot = jnp.take_along_axis(prior + before, ids_t, axis=1) + rank_local  34.9 us
    gather x1, local copies, waits for them, and re-layouts, device_step(): picked = jnp.take(returned, target, axis=0)  21.4 us
    psum x1, blocking collectives, device_step(): totals = lax.psum(counts, 'expert')  21.2 us
  transfers between devices with their start and end apart: 4, of which 2 were waited for; matrix products, arithmetic and copies ran while one was open for 8% of the time, Pallas kernels for 0%

commit v1 on v0

v1 whole, which is shorter than its diff:
```python
import functools

import jax
import jax.numpy as jnp
from jax import lax
from jax.experimental import pallas as pl
from jax.experimental.pallas import tpu as pltpu
from jax.sharding import PartitionSpec as P

GROUPS = 2
BUFS = 4
LANES = 128
MESH = pl.DeviceIdType.MESH


def route_local(expert_ids, experts):
    ids_t = expert_ids.T
    onehot = (ids_t[:, :, None] == jnp.arange(experts, dtype=jnp.int32)).astype(jnp.int32)
    running = jnp.cumsum(onehot, axis=1)
    counts = running[:, -1, :]
    rank_local = jnp.sum(onehot * running, axis=2) - 1
    return ids_t, counts, rank_local


def padded_step(groups, token_rows, expert_ids, gate_weights, w_in, w_out):
    tokens, top_k = expert_ids.shape
    local_experts, model_dim = w_in.shape[0], w_in.shape[1]
    experts = local_experts * groups
    mean_load = tokens * top_k // experts
    send_cap = 7 * mean_load // 4
    capacity = groups * mean_load
    rows_total = experts * send_cap
    ids_t, counts, rank_local = route_local(expert_ids, experts)
    inclusive = counts
    shift = 1
    while shift < groups:
        pairs_list = [(source, source + shift) for source in range(groups - shift)]
        inclusive = inclusive + lax.ppermute(inclusive, "expert", pairs_list)
        shift = shift * 2
    before = inclusive - counts
    totals = lax.psum(counts, "expert")
    prior = jnp.cumsum(totals, axis=0) - totals
    within = jnp.cumsum(counts, axis=0) - counts
    slot = jnp.take_along_axis(prior + before, ids_t, axis=1) + rank_local
    keep = slot < capacity
    target = ids_t * send_cap + jnp.take_along_axis(within, ids_t, axis=1) + rank_local
    token_ids = jnp.broadcast_to(jnp.arange(tokens, dtype=jnp.int32), (top_k, tokens))
    source_row = jnp.full((rows_total,), tokens, jnp.int32).at[jnp.where(keep, target, rows_total).reshape(-1)].set(token_ids.reshape(-1), mode="drop")
    padded = jnp.concatenate([token_rows, jnp.zeros((1, model_dim), token_rows.dtype)], axis=0)
    outbound = jnp.take(padded, source_row, axis=0).reshape(experts, send_cap, model_dim)
    inbound = lax.all_to_all(outbound, "expert", 0, 0, tiled=True).reshape(groups, local_experts, send_cap, model_dim)
    pre_act = jnp.einsum("gesd,edf->gesf", inbound, w_in, preferred_element_type=jnp.float32)
    hidden = jax.nn.gelu(pre_act).astype(jnp.bfloat16)
    expert_out = jnp.einsum("gesf,efd->gesd", hidden, w_out, preferred_element_type=jnp.float32).astype(jnp.bfloat16)
    returned = lax.all_to_all(expert_out.reshape(experts, send_cap, model_dim), "expert", 0, 0, tiled=True).reshape(rows_total, model_dim)
    picked = jnp.take(returned, target, axis=0)
    weight = jnp.where(keep, gate_weights.T, 0.0)
    mixed = jnp.sum(weight[:, :, None] * picked.astype(jnp.float32), axis=0)
    return (token_rows.astype(jnp.float32) + mixed).astype(jnp.bfloat16)


def block_rows(tokens, top_k, groups):
    mean = tokens * top_k // (groups * GROUPS)
    return (mean * 19 // 16 + 15) // 16 * 16


def dot_f32(a, b):
    return jnp.dot(a, b, preferred_element_type=jnp.float32)


def routing(groups, expert_ids, local_experts, capacity):
    tokens, top_k = expert_ids.shape
    experts = local_experts * groups
    group_experts = local_experts // GROUPS
    rows = block_rows(tokens, top_k, groups)
    positions = GROUPS * groups * rows
    me = lax.axis_index("expert")
    block = 256
    lane = jnp.arange(experts, dtype=jnp.int32)
    onehot = expert_ids.T[:, :, None] == lane
    onehot_b = onehot.astype(jnp.bfloat16).reshape(top_k, tokens // block, block, experts)
    tri = (jnp.arange(block)[:, None] > jnp.arange(block)[None, :]).astype(jnp.bfloat16)
    within = jnp.einsum("ab,jnbe->jnae", tri, onehot_b, preferred_element_type=jnp.float32)
    sums = jnp.sum(onehot_b.astype(jnp.float32), axis=2)
    base = jnp.cumsum(sums, axis=1) - sums
    counts = jnp.sum(sums, axis=1)
    everyone = lax.all_gather(counts, "expert")
    before = jnp.cumsum(everyone, axis=0) - everyone
    totals = jnp.sum(everyone, axis=0)
    prior = jnp.cumsum(totals, axis=0) - totals
    kept = jnp.clip(capacity - prior - before, 0.0, everyone)
    kept_all = jnp.sum(kept, axis=1)
    same = (lane[:, None] // group_experts == lane[None, :] // group_experts) & (lane[:, None] < lane[None, :])
    start = dot_f32(kept_all.astype(jnp.bfloat16), same.astype(jnp.bfloat16))
    overflow = jnp.max(start + kept_all) > rows
    block_of = (lane % local_experts // group_experts) * groups + lane // local_experts
    mine, mine_start = kept[me], start[me]
    first = (block_of * rows).astype(jnp.float32) + mine_start
    offset = jnp.stack([first, first + mine[0]])
    rank = within + base[:, :, None, :]
    value = jnp.where(rank < mine[:, None, None, :], rank + offset[:, None, None, :], float(positions))
    pos = jnp.sum(jnp.where(onehot.reshape(value.shape), value, 0.0), axis=3).reshape(top_k, tokens).astype(jnp.int32)
    high = (pos[:, :, None] // LANES == jnp.arange(positions // LANES, dtype=jnp.int32)).astype(jnp.bfloat16)
    low = pos[:, :, None] % LANES == jnp.arange(LANES, dtype=jnp.int32)
    token = jnp.arange(tokens, dtype=jnp.int32)[:, None]
    low_hi = jnp.where(low, (token // 8).astype(jnp.float32), 0.0).astype(jnp.bfloat16)
    low_lo = jnp.where(low, (token % 8).astype(jnp.float32), 0.0).astype(jnp.bfloat16)
    found = jnp.einsum("jth,jtl->hl", high, jnp.concatenate([low_hi, low_lo], axis=2), preferred_element_type=jnp.float32)
    pack = (found[:, :LANES] * 8.0 + found[:, LANES:]).astype(jnp.int32).reshape(-1)

    cum = jnp.cumsum(kept_all, axis=0) - kept_all
    local = lambda a: lax.dynamic_slice_in_dim(a, me * local_experts, local_experts, 1)
    k_l, s_l, c_l = local(kept_all), local(start), local(cum)
    q = jnp.arange(capacity, dtype=jnp.float32)[:, None]
    lhs = jnp.zeros((capacity, local_experts), jnp.float32)
    for s in range(groups):
        inside = (q >= c_l[s]) & (q < c_l[s] + k_l[s])
        lhs = lhs + jnp.where(inside, s * rows + s_l[s] - c_l[s] + q, 0.0)
    lhs = lhs.astype(jnp.int32).reshape(-1)

    in_group = (jnp.arange(local_experts, dtype=jnp.int32) % group_experts).astype(jnp.float32)
    v = in_group * capacity + c_l - s_l
    v = v.reshape(groups, GROUPS, group_experts)
    step = v - jnp.concatenate([jnp.zeros_like(v[:, :, :1]), v[:, :, :-1]], axis=2)
    p = jnp.arange(rows, dtype=jnp.float32)[:, None]
    reached = p >= s_l.reshape(groups, GROUPS, 1, group_experts)
    ret = p[:, 0] + jnp.sum(jnp.where(reached, step[:, :, None, :], 0.0), axis=3)
    ret = jnp.clip(ret, 0.0, group_experts * capacity - 1.0).astype(jnp.int32)
    ret = ret.transpose(1, 0, 2).reshape(-1)
    return overflow, pack, lhs, ret, pos.reshape(-1)


def exchange_kernel(
    groups, rows, capacity,
    pack_idx, lhs_idx, ret_idx, comb_idx, gates, x_ref, win_ref, wout_ref, out_ref,
    xr_rows, send, recv, rf_rows, stage0, stage1, of_rows, rsend, rrecv, retf_rows, wi, wo,
    wsem, ssem, rsem, rssem, rrsem,
):
    tokens, model_dim = x_ref.shape
    sub = model_dim // LANES
    local_experts = win_ref.shape[0]
    group_experts = local_experts // GROUPS
    me = lax.axis_index("expert")
    span = rows * sub
    stages = (stage0, stage1)
    xr, rf, of, retf = (r.reshape(r.shape[0] * sub, LANES) for r in (xr_rows, rf_rows, of_rows, retf_rows))

    def fetch(e, slot):
        a = pltpu.make_async_copy(win_ref.at[e], wi.at[slot], wsem.at[slot, 0])
        b = pltpu.make_async_copy(wout_ref.at[e], wo.at[slot], wsem.at[slot, 1])
        return a, b

    for e in range(BUFS):
        for c in fetch(e, e):
            c.start()
    barrier = pltpu.get_barrier_semaphore()
    for k in range(1, groups):
        pl.semaphore_signal(barrier, inc=1, device_id={"expert": lax.rem(me + k, groups)}, device_id_type=MESH)
    for k in range(sub):
        xr[pl.ds(k, tokens, stride=sub), :] = x_ref[:, k * LANES:(k + 1) * LANES].astype(jnp.float32)
    retf[pl.ds(GROUPS * groups * span, 8 * sub), :] = jnp.zeros((8 * sub, LANES), jnp.float32)
    pl.semaphore_wait(barrier, groups - 1)

    def gather_block(idx, first, table, dst):
        def body(c, carry):
            got = [table[idx[first + c * 16 + r]] for r in range(16)]
            dst[pl.ds(pl.multiple_of(c * 16 * sub, 16 * sub), 16 * sub), :] = jnp.concatenate(got, axis=0).astype(jnp.bfloat16)
            return carry
        lax.fori_loop(0, rows // 16, body, 0)

    def widen(src, dst, first):
        def body(c, carry):
            part = pl.multiple_of(c * 16 * sub, 16 * sub)
            dst[pl.ds(pl.multiple_of(first + part, 16), 16 * sub), :] = src[pl.ds(part, 16 * sub), :].astype(jnp.float32)
            return carry
        lax.fori_loop(0, rows // 16, body, 0)

    def copy_to(src, dst, g, k, s_sem, r_sem):
        peer = lax.rem(me + k, groups)
        return pltpu.make_async_remote_copy(
            src_ref=src.at[g, peer], dst_ref=dst.at[g, me], send_sem=s_sem.at[g, k], recv_sem=r_sem.at[g, k],
            device_id={"expert": peer}, device_id_type=MESH)

    def send_blocks(g, idx, table, src, dst, s_sem, r_sem):
        late = None
        for k in list(range(1, groups)) + [0]:
            peer = lax.rem(me + k, groups)
            gather_block(idx, (g * groups + peer) * rows, table, src.at[g, peer])
            if late is not None:
                late.start()
            late = copy_to(src, dst, g, k, s_sem, r_sem) if k else None

    def take_blocks(g, src, dst, own, first, s_sem, r_sem):
        for k in range(groups):
            peer = lax.rem(me - k + groups, groups)
            if k:
                pltpu.make_async_remote_copy(
                    src_ref=own.at[g, peer], dst_ref=src.at[g, peer], send_sem=s_sem.at[g, k], recv_sem=r_sem.at[g, k],
                    device_id={"expert": peer}, device_id_type=MESH).wait_recv()
                widen(src.at[g, peer], dst, first + peer * span)
            else:
                widen(own.at[g, peer], dst, first + peer * span)

    for g in range(GROUPS):
        send_blocks(g, pack_idx, xr_rows, send, recv, ssem, rsem)

    for g in range(GROUPS):
        take_blocks(g, recv, rf, send, 0, ssem, rsem)

        def gather_lhs(e, stage):
            for q in range(capacity):
                stage[pl.ds(q * sub, sub), :] = rf_rows[lhs_idx[q * local_experts + e]]

        def ffn(e, stage):
            slot = lax.rem(e, BUFS)
            for c in fetch(e, slot):
                c.wait()
            lhs = jnp.concatenate([stage[pl.ds(k, capacity, stride=sub), :] for k in range(sub)], axis=1).astype(jnp.bfloat16)
            hidden = jax.nn.gelu(dot_f32(lhs, wi[slot])).astype(jnp.bfloat16)
            out = dot_f32(hidden, wo[slot]).astype(jnp.bfloat16).astype(jnp.float32)
            at = (e - g * group_experts) * capacity * sub
            for k in range(sub):
                of[pl.ds(at + k, capacity, stride=sub), :] = out[:, k * LANES:(k + 1) * LANES]

        def body(i, carry):
            for half in range(2):
                e = g * group_experts + i * 2 + half
                gather_lhs(e, stages[half])
                ffn(e, stages[half])

                @pl.when(e + BUFS < local_experts)
                def _():
                    for c in fetch(e + BUFS, lax.rem(e, BUFS)):
                        c.start()
            return carry

        lax.fori_loop(0, group_experts // 2, body, 0)
        send_blocks(g, ret_idx, of_rows, rsend, rrecv, rssem, rrsem)

    for g in range(GROUPS):
        take_blocks(g, rrecv, retf, rsend, g * groups * span, rssem, rrsem)

    def combine(c, carry):
        got = []
        for r in range(16):
            t = c * 16 + r
            row = xr_rows[t]
            for j in range(2):
                row = row + gates[j * tokens + t] * retf_rows[comb_idx[j * tokens + t]]
            got.append(row)
        xr[pl.ds(pl.multiple_of(c * 16 * sub, 16 * sub), 16 * sub), :] = jnp.concatenate(got, axis=0)
        return carry

    lax.fori_loop(0, tokens // 16, combine, 0)
    for k in range(sub):
        out_ref[:, k * LANES:(k + 1) * LANES] = xr[pl.ds(k, tokens, stride=sub), :].astype(jnp.bfloat16)
    for g in range(GROUPS):
        for k in range(1, groups):
            copy_to(send, recv, g, k, ssem, rsem).wait_send()
            copy_to(rsend, rrecv, g, k, rssem, rrsem).wait_send()


def compact_step(groups, capacity, pack, lhs, ret, comb, gates, token_rows, w_in, w_out):
    tokens, model_dim = token_rows.shape
    local_experts, _, hidden_dim = w_in.shape
    group_experts = local_experts // GROUPS
    rows = pack.shape[0] // (GROUPS * groups)
    sub = model_dim // LANES
    span = rows * sub
    smem = pl.BlockSpec(memory_space=pltpu.SMEM)
    vmem = pl.BlockSpec(memory_space=pltpu.VMEM)
    hbm = pl.BlockSpec(memory_space=pl.ANY)
    wire = pltpu.VMEM((GROUPS, groups, span, LANES), jnp.bfloat16)
    sems = pltpu.SemaphoreType.DMA((GROUPS, groups))
    return pl.pallas_call(
        functools.partial(exchange_kernel, groups, rows, capacity),
        out_shape=jax.ShapeDtypeStruct((tokens, model_dim), jnp.bfloat16),
        in_specs=[smem] * 5 + [vmem, hbm, hbm],
        out_specs=vmem,
        scratch_shapes=[
            pltpu.VMEM((tokens, sub, LANES), jnp.float32),
            wire,
            wire,
            pltpu.VMEM((groups * rows, sub, LANES), jnp.float32),
            pltpu.VMEM((capacity * sub, LANES), jnp.float32),
            pltpu.VMEM((capacity * sub, LANES), jnp.float32),
            pltpu.VMEM((group_experts * capacity, sub, LANES), jnp.float32),
            wire,
            wire,
            pltpu.VMEM((GROUPS * groups * rows + 8, sub, LANES), jnp.float32),
            pltpu.VMEM((BUFS, model_dim, hidden_dim), jnp.bfloat16),
            pltpu.VMEM((BUFS, hidden_dim, model_dim), jnp.bfloat16),
            pltpu.SemaphoreType.DMA((BUFS, 2)),
            sems, sems, sems, sems,
        ],
        compiler_params=pltpu.CompilerParams(collective_id=0, has_side_effects=True, vmem_limit_bytes=64000000),
        name="expert_exchange",
    )(pack, lhs, ret, comb, gates, token_rows, w_in, w_out)


def solution(mesh):
    groups = mesh.shape["expert"]
    row_spec = P(("data", "expert"), None)
    weight_spec = P("expert", None, None)

    def device_step(token_rows, expert_ids, gate_weights, w_in, w_out):
        tokens, top_k = expert_ids.shape
        local_experts = w_in.shape[0]
        capacity = tokens * top_k // local_experts
        overflow, pack, lhs, ret, comb = routing(groups, expert_ids, local_experts, capacity)
        fast = compact_step(groups, capacity, pack, lhs, ret, comb, gate_weights.T.reshape(-1), token_rows, w_in, w_out)
        return lax.cond(
            overflow,
            lambda f: padded_step(groups, token_rows, expert_ids, gate_weights, w_in, w_out),
            lambda f: f,
            fast,
        )

    return jax.shard_map(device_step, mesh=mesh, in_specs=(row_spec, row_spec, row_spec, weight_spec, weight_spec), out_specs=row_spec, check_vma=False)
```

time: 489 us -> 154 us (0.31); the launches traced: 484 us -> 154 us
  local copies, waits for them, and re-layouts: 186 us -> 6.52 us
  Pallas kernels: 0 us -> 125 us
  blocking collectives: 119 us -> 11 us
  waiting for transfers between devices: 90.7 us -> 0 us
  matrix products: 51.2 us -> 5.18 us
  starting transfers between devices: 16.8 us -> 0 us
  other arithmetic: 19 us -> 5.23 us
    gather x7 -> x0, local copies, waits for them, and re-layouts: 133 us -> none  [the longest x2 41.4 us: device_step(): jnp.take(padded, source_row, axis=0).reshape(experts, send_cap, model_dim)]
    pallas_call x0 -> x1, Pallas kernels: none -> 125 us  [compact_step(): pl.pallas_call(functools.partial(exchange_kernel, groups, rows, capacity)...]
    all_to_all x1 -> x0, blocking collectives: 98.1 us -> none  [device_step(): lax.all_to_all(outbound, 'expert', 0, 0, tiled=True)]
    all_to_all x1 -> x0, waiting for transfers between devices: 90 us -> none  [device_step(): lax.all_to_all(expert_out.reshape(experts, send_cap, model_dim), 'expert'...]
    dot_general x1 -> x3, matrix products: 51.2 us -> 5.18 us  [the longest x1 3.8 us: routing(): jnp.einsum('ab,jnbe->jnae', tri, onehot_b, preferred_element_type=jnp.flo...]
    psum x1 -> x0, blocking collectives: 21.2 us -> none  [device_step(): totals = lax.psum(counts, 'expert')]
    reshape x2, local copies, waits for them, and re-layouts: 19.5 us -> 0.76 us  [the longest x1 0.68 us: routing(): ret = ret.transpose(1, 0, 2).reshape(-1)]
    scatter x1 -> x0, local copies, waits for them, and re-layouts: 15.7 us -> none  [device_step(): jnp.full((rows_total,), tokens, jnp.int32)]
  transfers between devices with their start and end apart: 4 -> 0, of which waited for: 2 -> 0; matrix products, arithmetic and copies ran while one was open for 8% -> 0% of each run, Pallas kernels for 0% -> 0%
where the time goes in v1:
time: 154 us
  Pallas kernels  125 us (81%)
  blocking collectives  11 us (7%)
  local copies, waits for them, and re-layouts  6.52 us (4%)
  other arithmetic  5.23 us (3%)
  matrix products  5.18 us (3%)
    pallas_call x1, Pallas kernels, compact_step(): pl.pallas_call(functools.partial(exchange_kernel, groups, rows, capacity)...  125 us
    all_gather x1, blocking collectives, routing(): everyone = lax.all_gather(counts, 'expert')  11 us
    unnamed x11, local copies, waits for them, and re-layouts  5 us
    dot_general x1, matrix products, routing(): jnp.einsum('ab,jnbe->jnae', tri, onehot_b, preferred_element_type=jnp.flo...  3.8 us

profile of v1, /device:TPU:1, one launch (start us, length us, event | category | flops | bytes accessed | tf_op | source)
XLA Modules:
  0.0 153.6 jit_solution(11829581888478499679)
XLA Ops:
  0.0 0.7 copy.78
  0.7 2.3 %convert_reduce_fusion = (f32[2,8,512]{2,1,0:T(8,128)S(1)}, f32[2,512]{1,0:T(2,128)S(1)}) fusion(s32[2,8,256]{2,1,0:T(8,128)S(1)} %bitcast.190), kind=kLoop, calls=%fused_computation.65 | loop fusion | flops 10476544 | bytes 53248 | tf_op jit(solution)/shard_map/reduce_sum | solution.py:84
  3.0 11.0 %all-gather.1 = f32[8,2,512]{2,1,0:T(2,128)S(1)} all-gather(f32[1,2,512]{2,1,0:T(2,128)S(1)} %bitcast.200), channel_id=2, replica_groups=mesh['data'=1,'expert'=8] {'expert'}, dimensions={0}, use_global_device_ids=true | all-gather | bytes 36864 | tf_op jit(solution)/shard_map/all_gather | solution.py:87
  14.1 0.1 fusion.104
  14.2 0.9 add_reduce_fusion
  15.1 0.1 add_subtract_fusion
  15.2 0.1 add_convert_fusion.1
  15.3 0.7 reshape.575.lhs_idx
  16.1 0.0 copy-start.5
  16.1 0.0 copy-start.1
  16.1 3.8 %fusion.50 = f32[2,8,256]{2,1,0:T(8,128)S(1)} fusion(f32[2,512]{1,0:T(2,128)S(1)} %pad_maximum_fusion, f32[2,512]{1,0:T(2,128)S(1)} %dynamic-slice_bitcast_fusion, f32[2,8,512]{2,1,0:T(8,128)S(1)} %sub.127, s32[2,8,256]{2,1,0:T(8,128)S(1)} %bitcast.191), kind=kOutput, calls=%fused_computation.68 | convolution fusion | flops 1090580480 | bytes 73728 | tf_op jit(solution)/shard_map/ab,jnbe->jnae/dot_general | solution.py:83
  20.0 0.1 and_select_fusion.1
  20.1 1.5 select_convert_fusion.1
  21.5 0.5 fusion.58
  22.0 0.6 fusion.83.pack_idx
  22.6 0.1 reshape.515
  22.7 0.1 pad_subtract_fusion
  22.8 0.1 ge.251
  22.8 0.3 select_reduce_fusion.1
  23.1 0.7 reshape.516.ret_idx
  23.8 0.6 copy.54
  24.4 0.0 copy-done.5
  24.4 0.6 copy.55
  25.0 0.0 copy-done.1
  25.0 0.0 copy-start.4
  25.0 124.7 %expert_exchange.1 = bf16[2048,512]{1,0:T(8,128)(2,1)} custom-call(s32[4864]{0:T(1024)} %fusion.83.pack_idx, s32[4096]{0:T(1024)} %reshape.575.lhs_idx, s32[4864]{0:T(1024)} %reshape.516.ret_idx, s32[4096]{0:T(1024)} %bitcast.186, f32[4096]{0:T(1024)} %bitcast.187, bf16[2048,512]{1,0:T(8,128)(2,1)S(1)} %copy-done.1, bf16[64,512,1024]{2,1,0:T(8,128)(2,1)} %win_ref.1, ...), custom_call_target="tpu_custom_call" | custom-call | tf_op jit(solution)/shard_map/expert_exchange/pallas_call | solution.py:275
  150.3 0.0 copy-done.4
  150.3 0.2 conditional.1
  150.6 3.0 %copy.82 = bf16[2048,512]{1,0:T(8,128)(2,1)} copy(bf16[2048,512]{1,0:T(8,128)(2,1)} %get-tuple-element.25) | data formatting | bytes 4194304
  (18 shorter events, 0.3 us)
Async XLA Ops:
  16.1 8.3 %copy-start.5 = (f32[2048,2]{0,1:T(2,128)S(1)}, f32[2048,2]{0,1:T(2,128)}, u32[]{:S(2)}) copy-start(f32[2048,2]{0,1:T(2,128)} %param.11) | copy-start | bytes 49156
  16.1 8.9 %copy-start.1 = (bf16[2048,512]{1,0:T(8,128)(2,1)S(1)}, bf16[2048,512]{1,0:T(8,128)(2,1)}, u32[]{:S(2)}) copy-start(bf16[2048,512]{1,0:T(8,128)(2,1)} %x_ref.1) | copy-start | bytes 6291460
  25.0 125.3 %copy-start.4 = (s32[2048,2]{0,1:T(2,128)S(1)}, s32[2048,2]{0,1:T(2,128)}, u32[]{:S(2)}) copy-start(s32[2048,2]{0,1:T(2,128)} %param.10) | copy-start | bytes 49156

commit v2 on v1

v2 whole, which is shorter than its diff:
```python
import functools

import jax
import jax.numpy as jnp
from jax import lax
from jax.experimental import pallas as pl
from jax.experimental.pallas import tpu as pltpu
from jax.sharding import PartitionSpec as P

GROUPS = 2
BUFS = 3
LANES = 128
MESH = pl.DeviceIdType.MESH


def route_local(expert_ids, experts):
    ids_t = expert_ids.T
    onehot = (ids_t[:, :, None] == jnp.arange(experts, dtype=jnp.int32)).astype(jnp.int32)
    running = jnp.cumsum(onehot, axis=1)
    counts = running[:, -1, :]
    rank_local = jnp.sum(onehot * running, axis=2) - 1
    return ids_t, counts, rank_local


def padded_step(groups, token_rows, expert_ids, gate_weights, w_in, w_out):
    tokens, top_k = expert_ids.shape
    local_experts, model_dim = w_in.shape[0], w_in.shape[1]
    experts = local_experts * groups
    mean_load = tokens * top_k // experts
    send_cap = -(-(7 * mean_load // 4) // 16) * 16
    capacity = groups * mean_load
    rows_total = experts * send_cap
    ids_t, counts, rank_local = route_local(expert_ids, experts)
    inclusive = counts
    shift = 1
    while shift < groups:
        pairs_list = [(source, source + shift) for source in range(groups - shift)]
        inclusive = inclusive + lax.ppermute(inclusive, "expert", pairs_list)
        shift = shift * 2
    before = inclusive - counts
    totals = lax.psum(counts, "expert")
    prior = jnp.cumsum(totals, axis=0) - totals
    within = jnp.cumsum(counts, axis=0) - counts
    slot = jnp.take_along_axis(prior + before, ids_t, axis=1) + rank_local
    keep = slot < capacity
    target = ids_t * send_cap + jnp.take_along_axis(within, ids_t, axis=1) + rank_local
    token_ids = jnp.broadcast_to(jnp.arange(tokens, dtype=jnp.int32), (top_k, tokens))
    source_row = jnp.full((rows_total,), tokens, jnp.int32).at[jnp.where(keep, target, rows_total).reshape(-1)].set(token_ids.reshape(-1), mode="drop")
    padded = jnp.concatenate([token_rows, jnp.zeros((1, model_dim), token_rows.dtype)], axis=0)
    outbound = jnp.take(padded, source_row, axis=0).reshape(experts, send_cap, model_dim)
    inbound = lax.all_to_all(outbound, "expert", 0, 0, tiled=True).reshape(groups, local_experts, send_cap, model_dim)

    def one_expert(e, total):
        rows = lax.dynamic_index_in_dim(inbound, e, 1, keepdims=False).reshape(groups * send_cap, model_dim)
        hidden = jax.nn.gelu(jnp.dot(rows, w_in[e], preferred_element_type=jnp.float32)).astype(jnp.bfloat16)
        out = jnp.dot(hidden, w_out[e], preferred_element_type=jnp.float32).astype(jnp.bfloat16)
        return lax.dynamic_update_index_in_dim(total, out.reshape(groups, send_cap, model_dim), e, 1)

    expert_out = lax.fori_loop(0, local_experts, one_expert, jnp.zeros_like(inbound))
    returned = lax.all_to_all(expert_out.reshape(experts, send_cap, model_dim), "expert", 0, 0, tiled=True).reshape(rows_total, model_dim)
    picked = jnp.take(returned, target, axis=0)
    weight = jnp.where(keep, gate_weights.T, 0.0)
    mixed = jnp.sum(weight[:, :, None] * picked.astype(jnp.float32), axis=0)
    return (token_rows.astype(jnp.float32) + mixed).astype(jnp.bfloat16)


def block_rows(tokens, top_k, groups):
    mean = tokens * top_k // (groups * GROUPS)
    return (mean * 19 // 16 + 15) // 16 * 16


def dot_f32(a, b):
    return jnp.dot(a, b, preferred_element_type=jnp.float32)


def dot_nt(a, b):
    return lax.dot_general(a, b, (((1,), (1,)), ((), ())), preferred_element_type=jnp.float32)


def iota(shape, axis):
    return lax.broadcasted_iota(jnp.int32, shape, axis)


def as_bf16(mask):
    return jnp.where(mask, 1.0, 0.0).astype(jnp.bfloat16)


def pad_rows(rows, total):
    have = sum(r.shape[0] for r in rows)
    if have < total:
        rows = rows + [jnp.zeros((total - have, rows[0].shape[1]), rows[0].dtype)]
    return jnp.concatenate(rows, axis=0)


def local_positions(groups, rows, group_experts, ids_ref, hot, same, count_ref, rank_ref, pos_ref, pack_ref):
    tokens = ids_ref.shape[1]
    experts = hot.shape[1]
    blocks = tokens // LANES
    local_experts = experts // groups

    def fill(b, carry):
        at = pl.ds(pl.multiple_of(b * LANES, LANES), LANES)
        for j in range(2):
            hot[j, :, at] = as_bf16(iota((experts, LANES), 0) == ids_ref[j:j + 1, at])
        return carry

    lax.fori_loop(0, blocks, fill, 0)
    part = as_bf16(iota((blocks, tokens), 0) == iota((blocks, tokens), 1) // LANES)
    below = as_bf16(iota((blocks, blocks), 0) > iota((blocks, blocks), 1))
    base, count = [], []
    for j in range(2):
        per_block = dot_nt(part, hot[j])
        base.append(dot_f32(below, per_block.astype(jnp.bfloat16)))
        count.append(jnp.sum(per_block, axis=0, keepdims=True))
    count_ref[...] = pad_rows(count, 8)
    return base, count


def place_pairs(groups, rows, group_experts, base, count, ids_ref, hot, same, rank_ref, pos_ref, pack_ref):
    tokens = ids_ref.shape[1]
    experts = hot.shape[1]
    blocks = tokens // LANES
    local_experts = experts // groups
    both = pad_rows([count[0] + count[1]], 8)
    start = dot_f32(both.astype(jnp.bfloat16), same[...])[0:1]
    lane = iota((1, experts), 1)
    block_of = (lane % local_experts // group_experts) * groups + lane // local_experts
    first = (block_of * rows).astype(jnp.float32) + start
    earlier = iota((LANES, LANES), 0) < iota((LANES, LANES), 1)
    found = None
    table_rows = pack_ref.shape[0]
    for j in range(2):
        at = first if j == 0 else first + count[0]
        high = jnp.floor(at * (1.0 / 64.0))
        look = dot_f32(pad_rows([base[j], high, at - 64.0 * high], 32).astype(jnp.bfloat16), hot[j])
        for b in range(blocks):
            cols = slice(b * LANES, (b + 1) * LANES)
            row = ids_ref[j:j + 1, cols]
            wide = jnp.broadcast_to(row.astype(jnp.float32), (LANES, LANES))
            same_id = (wide.T == wide) & earlier
            rank = jnp.sum(jnp.where(same_id, 1.0, 0.0), axis=0, keepdims=True) + look[b:b + 1, cols]
            rank_ref[j:j + 1, cols] = rank
            pos_ref[j:j + 1, cols] = rank + 64.0 * look[blocks:blocks + 1, cols] + look[blocks + 1:blocks + 2, cols]
        pos = pos_ref[j:j + 1, :].astype(jnp.int32)
        token = iota((LANES, tokens), 1)
        high_t = as_bf16(iota((table_rows, tokens), 0) == pos // LANES)
        low = iota((LANES, tokens), 0) == pos % LANES
        low_hi = jnp.where(low, (token // 8).astype(jnp.float32), 0.0).astype(jnp.bfloat16)
        low_lo = jnp.where(low, (token % 8).astype(jnp.float32), 0.0).astype(jnp.bfloat16)
        hit = 8.0 * dot_nt(high_t, low_hi) + dot_nt(high_t, low_lo)
        found = hit if found is None else found + hit
    pack_ref[...] = jnp.clip(found.astype(jnp.int32), 0, tokens - 1)


def group_tables(me, groups, rows, group_experts, capacity, every, hot, same, rank_ref, pos_ref, lhs_ref, ret_ref, comb_ref, load_ref):
    experts = hot.shape[1]
    tokens = hot.shape[2]
    local_experts = experts // groups
    blocks = tokens // LANES
    c = [[every[s, j:j + 1, :] for s in range(groups)] for j in range(2)]
    both = pad_rows([c[0][s] + c[1][s] for s in range(groups)], 8)
    start = dot_f32(both.astype(jnp.bfloat16), same[...])
    load_ref[...] = jnp.broadcast_to(jnp.max(start + both), load_ref.shape)
    kept = [[None] * groups, [None] * groups]
    used = jnp.zeros((1, experts), jnp.float32)
    for j in range(2):
        for s in range(groups):
            kept[j][s] = jnp.clip(capacity - used, 0.0, c[j][s])
            used = used + c[j][s]
    lane = iota((1, experts), 1)
    in_group = lane % group_experts
    slot = jnp.zeros((1, experts), jnp.float32)
    slots, steps, edges, jumps = [], [], [], []
    last = jnp.zeros((1, experts), jnp.float32)
    for s in range(groups):
        ret_v = []
        for j in range(2):
            edge = start[s:s + 1] if j == 0 else start[s:s + 1] + c[0][s]
            v = s * rows + edge - slot
            slots.append(slot)
            steps.append(v - last)
            last = v
            edges.append(edge)
            ret_v.append((in_group * capacity).astype(jnp.float32) + slot - edge)
            slot = slot + kept[j][s]
        before = jnp.concatenate([jnp.zeros((1, 1), jnp.float32), ret_v[1][:, :-1]], axis=1)
        jumps.append(ret_v[0] - jnp.where(in_group == 0, 0.0, before))
        jumps.append(ret_v[1] - ret_v[0])

    def mine(parts):
        a = jnp.concatenate(parts, axis=0)
        total = jnp.zeros((a.shape[0], local_experts), jnp.float32)
        for d in range(groups):
            total = total + jnp.where(me == d, a[:, d * local_experts:(d + 1) * local_experts], 0.0)
        return total

    slots, steps, edges, jumps = mine(slots), mine(steps), mine(edges), mine(jumps)
    q = iota((capacity, local_experts), 0).astype(jnp.float32)
    lhs = q
    for i in range(2 * groups):
        lhs = lhs + jnp.where(q >= slots[i:i + 1], steps[i:i + 1], 0.0)
    lhs = jnp.clip(lhs.astype(jnp.int32), 0, groups * rows - 1)
    lhs_ref[...] = jnp.concatenate([lhs, jnp.zeros((capacity, LANES - local_experts), jnp.int32)], axis=1) if local_experts < LANES else lhs

    tall = pad_rows([edges, jumps], LANES)
    tall = jnp.concatenate([tall, jnp.zeros((LANES, LANES - local_experts), jnp.float32)], axis=1).T if local_experts < LANES else tall.T
    width = -(-rows // LANES) * LANES
    p = iota((1, width), 1).astype(jnp.float32)
    for g in range(GROUPS):
        part = tall[g * group_experts:(g + 1) * group_experts]
        for s in range(groups):
            total = jnp.zeros((group_experts, width), jnp.float32)
            for j in range(2):
                i = 2 * s + j
                total = total + jnp.where(p >= part[:, i:i + 1], part[:, 2 * groups + i:2 * groups + i + 1], 0.0)
            row = p + jnp.sum(total, axis=0, keepdims=True)
            row = jnp.clip(row.astype(jnp.int32), 0, group_experts * capacity - 1)
            for i in range(width // LANES):
                at = (g * groups + s) * (width // LANES) + i
                ret_ref[at:at + 1, :] = row[:, i * LANES:(i + 1) * LANES]

    for j in range(2):
        own = jnp.zeros((1, experts), jnp.float32)
        for s in range(groups):
            own = own + jnp.where(me == s, kept[j][s], 0.0)
        bound = dot_f32(pad_rows([own], 16).astype(jnp.bfloat16), hot[j])
        none = float(GROUPS * groups * rows)
        for b in range(blocks):
            cols = slice(b * LANES, (b + 1) * LANES)
            take = jnp.where(rank_ref[j:j + 1, cols] < bound[0:1, cols], pos_ref[j:j + 1, cols], none)
            comb_ref[j * blocks + b:j * blocks + b + 1, :] = jnp.clip(take.astype(jnp.int32), 0, GROUPS * groups * rows)


def exchange_kernel(
    groups, rows, capacity,
    gates, ids_ref, x_ref, win_ref, wout_ref, out_ref, load_ref,
    hot, same, count, every, rank_ref, pos_ref, pack_v, lhs_v, ret_v, comb_v, pack_idx, lhs_idx, ret_idx, comb_idx,
    xr_rows, send, recv, rf_rows, stage0, stage1, of_rows, rsend, rrecv, retf_rows, wi, wo,
    wsem, ssem, rsem, rssem, rrsem, csend, crecv, tsem,
):
    tokens, model_dim = x_ref.shape
    sub = model_dim // LANES
    local_experts = win_ref.shape[0]
    group_experts = local_experts // GROUPS
    me = lax.axis_index("expert")
    span = rows * sub
    stages = (stage0, stage1)
    xr, rf, of, retf = (r.reshape(r.shape[0] * sub, LANES) for r in (xr_rows, rf_rows, of_rows, retf_rows))

    def fetch(e, slot):
        a = pltpu.make_async_copy(win_ref.at[e], wi.at[slot], wsem.at[slot, 0])
        b = pltpu.make_async_copy(wout_ref.at[e], wo.at[slot], wsem.at[slot, 1])
        return a, b

    for e in range(BUFS):
        for c in fetch(e, e):
            c.start()
    barrier = pltpu.get_barrier_semaphore()
    for k in range(1, groups):
        pl.semaphore_signal(barrier, inc=1, device_id={"expert": lax.rem(me + k, groups)}, device_id_type=MESH)
    for k in range(sub):
        xr[pl.ds(k, tokens, stride=sub), :] = x_ref[:, k * LANES:(k + 1) * LANES].astype(jnp.float32)
    retf[pl.ds(GROUPS * groups * span, 8 * sub), :] = jnp.zeros((8 * sub, LANES), jnp.float32)
    experts = hot.shape[1]
    i_e, i_f = iota((experts, experts), 0), iota((experts, experts), 1)
    same[...] = as_bf16((i_e // group_experts == i_f // group_experts) & (i_e < i_f))
    base, counts = local_positions(groups, rows, group_experts, ids_ref, hot, same, count, rank_ref, pos_ref, pack_v)
    place_pairs(groups, rows, group_experts, base, counts, ids_ref, hot, same, rank_ref, pos_ref, pack_v)
    pack_copy = pltpu.make_async_copy(pack_v, pack_idx, tsem.at[0])
    pack_copy.start()
    pl.semaphore_wait(barrier, groups - 1)

    def count_copy(k):
        return pltpu.make_async_remote_copy(
            src_ref=count, dst_ref=every.at[me], send_sem=csend.at[k], recv_sem=crecv.at[k],
            device_id={"expert": lax.rem(me + k, groups)}, device_id_type=MESH)

    for k in range(1, groups):
        count_copy(k).start()
    pack_copy.wait()

    def gather_block(idx, first, table, dst):
        def body(c, carry):
            at = first + c * 16
            line, col = at // LANES, at % LANES
            got = [table[idx[line, col + r]] for r in range(16)]
            dst[pl.ds(pl.multiple_of(c * 16 * sub, 16 * sub), 16 * sub), :] = jnp.concatenate(got, axis=0).astype(jnp.bfloat16)
            return carry
        lax.fori_loop(0, rows // 16, body, 0)

    def widen(src, dst, first):
        def body(c, carry):
            part = pl.multiple_of(c * 16 * sub, 16 * sub)
            dst[pl.ds(pl.multiple_of(first + part, 16), 16 * sub), :] = src[pl.ds(part, 16 * sub), :].astype(jnp.float32)
            return carry
        lax.fori_loop(0, rows // 16, body, 0)

    def copy_to(src, dst, g, k, s_sem, r_sem):
        peer = lax.rem(me + k, groups)
        return pltpu.make_async_remote_copy(
            src_ref=src.at[g, peer], dst_ref=dst.at[g, me], send_sem=s_sem.at[g, k], recv_sem=r_sem.at[g, k],
            device_id={"expert": peer}, device_id_type=MESH)

    def send_blocks(g, idx, stride, table, src, dst, s_sem, r_sem):
        late = None
        for k in list(range(1, groups)) + [0]:
            peer = lax.rem(me + k, groups)
            gather_block(idx, (g * groups + peer) * stride, table, src.at[g, peer])
            if late is not None:
                late.start()
            late = copy_to(src, dst, g, k, s_sem, r_sem) if k else None

    def take_blocks(g, src, dst, own, first, s_sem, r_sem):
        for k in range(groups):
            peer = lax.rem(me - k + groups, groups)
            if k:
                pltpu.make_async_remote_copy(
                    src_ref=own.at[g, peer], dst_ref=src.at[g, peer], send_sem=s_sem.at[g, k], recv_sem=r_sem.at[g, k],
                    device_id={"expert": peer}, device_id_type=MESH).wait_recv()
                widen(src.at[g, peer], dst, first + peer * span)
            else:
                widen(own.at[g, peer], dst, first + peer * span)

    for g in range(GROUPS):
        send_blocks(g, pack_idx, rows, xr_rows, send, recv, ssem, rsem)

    every[me] = count[...]
    for k in range(1, groups):
        source = lax.rem(me - k + groups, groups)
        pltpu.make_async_remote_copy(
            src_ref=count, dst_ref=every.at[source], send_sem=csend.at[k], recv_sem=crecv.at[k],
            device_id={"expert": source}, device_id_type=MESH).wait_recv()
    group_tables(me, groups, rows, group_experts, capacity, every, hot, same, rank_ref, pos_ref, lhs_v, ret_v, comb_v, load_ref)
    tables = [pltpu.make_async_copy(a, b, tsem.at[i + 1]) for i, (a, b) in enumerate(((lhs_v, lhs_idx), (ret_v, ret_idx), (comb_v, comb_idx)))]
    for t in tables:
        t.start()
    for t in tables:
        t.wait()

    for g in range(GROUPS):
        take_blocks(g, recv, rf, send, 0, ssem, rsem)

        def gather_lhs(e, stage):
            for q in range(capacity):
                stage[pl.ds(q * sub, sub), :] = rf_rows[lhs_idx[q, e]]

        def ffn(e, stage):
            slot = lax.rem(e, BUFS)
            for c in fetch(e, slot):
                c.wait()
            lhs = jnp.concatenate([stage[pl.ds(k, capacity, stride=sub), :] for k in range(sub)], axis=1).astype(jnp.bfloat16)
            hidden = jax.nn.gelu(dot_f32(lhs, wi[slot])).astype(jnp.bfloat16)
            out = dot_f32(hidden, wo[slot]).astype(jnp.bfloat16).astype(jnp.float32)
            at = (e - g * group_experts) * capacity * sub
            for k in range(sub):
                of[pl.ds(at + k, capacity, stride=sub), :] = out[:, k * LANES:(k + 1) * LANES]

        def body(i, carry):
            for half in range(2):
                e = g * group_experts + i * 2 + half
                gather_lhs(e, stages[half])
                ffn(e, stages[half])

                @pl.when(e + BUFS < local_experts)
                def _():
                    for c in fetch(e + BUFS, lax.rem(e, BUFS)):
                        c.start()
            return carry

        lax.fori_loop(0, group_experts // 2, body, 0)
        send_blocks(g, ret_idx, -(-rows // LANES) * LANES, of_rows, rsend, rrecv, rssem, rrsem)

    for g in range(GROUPS):
        take_blocks(g, rrecv, retf, rsend, g * groups * span, rssem, rrsem)

    def combine(c, carry):
        got = []
        line, col = c // (LANES // 16), c % (LANES // 16) * 16
        for r in range(16):
            row = xr_rows[c * 16 + r]
            for j in range(2):
                row = row + gates[j * (tokens // LANES) + line, col + r] * retf_rows[comb_idx[j * (tokens // LANES) + line, col + r]]
            got.append(row)
        xr[pl.ds(pl.multiple_of(c * 16 * sub, 16 * sub), 16 * sub), :] = jnp.concatenate(got, axis=0)
        return carry

    lax.fori_loop(0, tokens // 16, combine, 0)
    for k in range(sub):
        out_ref[:, k * LANES:(k + 1) * LANES] = xr[pl.ds(k, tokens, stride=sub), :].astype(jnp.bfloat16)
    for g in range(GROUPS):
        for k in range(1, groups):
            if g == 0:
                count_copy(k).wait_send()
            copy_to(send, recv, g, k, ssem, rsem).wait_send()
            copy_to(rsend, rrecv, g, k, rssem, rrsem).wait_send()


def compact_step(groups, rows, capacity, gates, ids, token_rows, w_in, w_out):
    tokens, model_dim = token_rows.shape
    local_experts, _, hidden_dim = w_in.shape
    experts = local_experts * groups
    group_experts = local_experts // GROUPS
    sub = model_dim // LANES
    span = rows * sub
    smem = pl.BlockSpec(memory_space=pltpu.SMEM)
    vmem = pl.BlockSpec(memory_space=pltpu.VMEM)
    hbm = pl.BlockSpec(memory_space=pl.ANY)
    wire = pltpu.VMEM((GROUPS, groups, span, LANES), jnp.bfloat16)
    sems = pltpu.SemaphoreType.DMA((GROUPS, groups))
    table_rows = (
        -(-(GROUPS * groups * rows) // (8 * LANES)) * 8,
        capacity,
        GROUPS * groups * -(-rows // LANES),
        2 * tokens // LANES,
    )
    return pl.pallas_call(
        functools.partial(exchange_kernel, groups, rows, capacity),
        out_shape=(jax.ShapeDtypeStruct((tokens, model_dim), jnp.bfloat16), jax.ShapeDtypeStruct((8, LANES), jnp.float32)),
        in_specs=[smem, vmem, vmem, hbm, hbm],
        out_specs=(vmem, vmem),
        scratch_shapes=[
            pltpu.VMEM((2, experts, tokens), jnp.bfloat16),
            pltpu.VMEM((experts, experts), jnp.bfloat16),
            pltpu.VMEM((8, experts), jnp.float32),
            pltpu.VMEM((groups, 8, experts), jnp.float32),
            pltpu.VMEM((8, tokens), jnp.float32),
            pltpu.VMEM((8, tokens), jnp.float32),
            *[pltpu.VMEM((r, LANES), jnp.int32) for r in table_rows],
            *[pltpu.SMEM((r, LANES), jnp.int32) for r in table_rows],
            pltpu.VMEM((tokens, sub, LANES), jnp.float32),
            wire,
            wire,
            pltpu.VMEM((groups * rows, sub, LANES), jnp.float32),
            pltpu.VMEM((capacity * sub, LANES), jnp.float32),
            pltpu.VMEM((capacity * sub, LANES), jnp.float32),
            pltpu.VMEM((group_experts * capacity, sub, LANES), jnp.float32),
            wire,
            wire,
            pltpu.VMEM((GROUPS * groups * rows + 8, sub, LANES), jnp.float32),
            pltpu.VMEM((BUFS, model_dim, hidden_dim), jnp.bfloat16),
            pltpu.VMEM((BUFS, hidden_dim, model_dim), jnp.bfloat16),
            pltpu.SemaphoreType.DMA((BUFS, 2)),
            sems, sems, sems, sems,
            pltpu.SemaphoreType.DMA((groups,)),
            pltpu.SemaphoreType.DMA((groups,)),
            pltpu.SemaphoreType.DMA((4,)),
        ],
        compiler_params=pltpu.CompilerParams(collective_id=0, has_side_effects=True, vmem_limit_bytes=67043328),
        name="expert_exchange",
    )(gates, ids, token_rows, w_in, w_out)


def solution(mesh):
    groups = mesh.shape["expert"]
    row_spec = P(("data", "expert"), None)
    weight_spec = P("expert", None, None)

    def device_step(token_rows, expert_ids, gate_weights, w_in, w_out):
        tokens, top_k = expert_ids.shape
        local_experts = w_in.shape[0]
        capacity = tokens * top_k // local_experts
        rows = block_rows(tokens, top_k, groups)
        gates = gate_weights.T.reshape(-1, LANES)
        fast, load = compact_step(groups, rows, capacity, gates, expert_ids.T, token_rows, w_in, w_out)
        overflow = load[0, 0] > rows
        return lax.cond(
            overflow,
            lambda f: padded_step(groups, token_rows, expert_ids, gate_weights, w_in, w_out),
            lambda f: f,
            fast,
        )

    return jax.shard_map(device_step, mesh=mesh, in_specs=(row_spec, row_spec, row_spec, weight_spec, weight_spec), out_specs=row_spec, check_vma=False)
```

time: 154 us -> 142 us (0.922)
  blocking collectives: 11 us -> 0 us
  Pallas kernels: 125 us -> 134 us
  other arithmetic: 5.23 us -> 0 us
  matrix products: 5.18 us -> 0 us
    all_gather x1 -> x0, blocking collectives: 11 us -> none  [routing(): everyone = lax.all_gather(counts, 'expert')]
    pallas_call x1, Pallas kernels: 125 us -> 134 us  [compact_step(): pl.pallas_call(functools.partial(exchange_kernel, groups, rows, capacity)...]
    dot_general x3 -> x0, matrix products: 5.18 us -> none  [the longest x1 3.8 us: routing(): jnp.einsum('ab,jnbe->jnae', tri, onehot_b, preferred_element_type=jnp.flo...]
    reduce_sum x3 -> x0, other arithmetic: 2.58 us -> none  [the longest x1 2.28 us: routing(): sums = jnp.sum(onehot_b.astype(jnp.float32), axis=2)]
    unnamed x11 -> x1, local copies, waits for them, and re-layouts: 5 us -> 3.05 us
    convert_element_type x4 -> x0, other arithmetic: 1.56 us -> none  [the longest x1 1.46 us: routing(): jnp.where(low, (token // 8).astype(jnp.float32), 0.0).astype(jnp.bfloat16)]
where the time goes in v2:
time: 142 us; the launch traced here: 140 us
  Pallas kernels  134 us (94%)
  local copies, waits for them, and re-layouts  5.57 us (4%)
    pallas_call x1, Pallas kernels, compact_step(): pl.pallas_call(functools.partial(exchange_kernel, groups, rows, capacity)...  134 us
    unnamed x1, local copies, waits for them, and re-layouts  3.05 us

profile of v2, /device:TPU:1, one launch (start us, length us, event | category | flops | bytes accessed | tf_op | source)
XLA Modules:
  0.0 140.5 jit_solution(8618077522002134018)
XLA Ops:
  0.0 1.3 reshape.100.gates
  1.3 134.0 %expert_exchange.1 = (bf16[2048,512]{1,0:T(8,128)(2,1)}, f32[8,128]{1,0:T(8,128)}) custom-call(f32[32,128]{1,0:T(8,128)} %reshape.100.gates, s32[2,2048]{1,0:T(2,128)} %bitcast.95, bf16[2048,512]{1,0:T(8,128)(2,1)} %x_ref.1, bf16[64,512,1024]{2,1,0:T(8,128)(2,1)} %win_ref.1, bf16[64,1024,512]{2,1,0:T(8,128)(2,1)} %wout_ref.1), custom_call_target="tpu_custom_call" | custom-call | tf_op jit(solution)/shard_map/expert_exchange/pallas_call | solution.py:416
  135.3 1.2 slice.12
  137.2 0.2 conditional.1
  137.4 3.0 %copy.43 = bf16[2048,512]{1,0:T(8,128)(2,1)} copy(bf16[2048,512]{1,0:T(8,128)(2,1)} %get-tuple-element.123) | data formatting | bytes 4194304

commit v3 on v2

--- a/solution.py
+++ b/solution.py
@@ -125,7 +125,8 @@
     start = dot_f32(both.astype(jnp.bfloat16), same[...])[0:1]
     lane = iota((1, experts), 1)
     block_of = (lane % local_experts // group_experts) * groups + lane // local_experts
-    first = (block_of * rows).astype(jnp.float32) + start
+    stride = -(-rows // LANES) * LANES
+    first = (block_of * stride).astype(jnp.float32) + start
     earlier = iota((LANES, LANES), 0) < iota((LANES, LANES), 1)
     found = None
     table_rows = pack_ref.shape[0]
@@ -141,7 +142,9 @@
             rank = jnp.sum(jnp.where(same_id, 1.0, 0.0), axis=0, keepdims=True) + look[b:b + 1, cols]
             rank_ref[j:j + 1, cols] = rank
             pos_ref[j:j + 1, cols] = rank + 64.0 * look[blocks:blocks + 1, cols] + look[blocks + 1:blocks + 2, cols]
-        pos = pos_ref[j:j + 1, :].astype(jnp.int32)
+        pos = pos_ref[j:j + 1, :]
+        pos_ref[j:j + 1, :] = pos - (stride - rows) * jnp.floor((pos + 0.5) * (1.0 / stride))
+        pos = pos.astype(jnp.int32)
         token = iota((LANES, tokens), 1)
         high_t = as_bf16(iota((table_rows, tokens), 0) == pos // LANES)
         low = iota((LANES, tokens), 0) == pos % LANES
@@ -195,15 +198,15 @@
         return total
 
     slots, steps, edges, jumps = mine(slots), mine(steps), mine(edges), mine(jumps)
-    q = iota((capacity, local_experts), 0).astype(jnp.float32)
+    tall = pad_rows([edges, jumps, slots, steps], LANES)
+    tall = jnp.concatenate([tall, jnp.zeros((LANES, LANES - local_experts), jnp.float32)], axis=1).T if local_experts < LANES else tall.T
+    q = iota((local_experts, LANES), 1).astype(jnp.float32)
     lhs = q
     for i in range(2 * groups):
-        lhs = lhs + jnp.where(q >= slots[i:i + 1], steps[i:i + 1], 0.0)
-    lhs = jnp.clip(lhs.astype(jnp.int32), 0, groups * rows - 1)
-    lhs_ref[...] = jnp.concatenate([lhs, jnp.zeros((capacity, LANES - local_experts), jnp.int32)], axis=1) if local_experts < LANES else lhs
-
-    tall = pad_rows([edges, jumps], LANES)
-    tall = jnp.concatenate([tall, jnp.zeros((LANES, LANES - local_experts), jnp.float32)], axis=1).T if local_experts < LANES else tall.T
+        at = 4 * groups + i
+        lhs = lhs + jnp.where(q >= tall[:local_experts, at:at + 1], tall[:local_experts, at + 2 * groups:at + 2 * groups + 1], 0.0)
+    lhs_ref[...] = jnp.clip(lhs.astype(jnp.int32), 0, groups * rows - 1)
+
     width = -(-rows // LANES) * LANES
     p = iota((1, width), 1).astype(jnp.float32)
     for g in range(GROUPS):
@@ -233,8 +236,8 @@
 
 def exchange_kernel(
     groups, rows, capacity,
-    gates, ids_ref, x_ref, win_ref, wout_ref, out_ref, load_ref,
-    hot, same, count, every, rank_ref, pos_ref, pack_v, lhs_v, ret_v, comb_v, pack_idx, lhs_idx, ret_idx, comb_idx,
+    gates_ref, ids_ref, x_ref, win_ref, wout_ref, out_ref, load_ref,
+    hot, same, count, every, rank_ref, pos_ref, pack_v, lhs_v, ret_v, comb_v, gates_v, pack_idx, lhs_idx, ret_idx, comb_idx, gates,
     xr_rows, send, recv, rf_rows, stage0, stage1, of_rows, rsend, rrecv, retf_rows, wi, wo,
     wsem, ssem, rsem, rssem, rrsem, csend, crecv, tsem,
 ):
@@ -279,14 +282,21 @@
         count_copy(k).start()
     pack_copy.wait()
 
-    def gather_block(idx, first, table, dst):
-        def body(c, carry):
-            at = first + c * 16
-            line, col = at // LANES, at % LANES
-            got = [table[idx[line, col + r]] for r in range(16)]
-            dst[pl.ds(pl.multiple_of(c * 16 * sub, 16 * sub), 16 * sub), :] = jnp.concatenate(got, axis=0).astype(jnp.bfloat16)
+    lines, rest = divmod(rows, LANES)
+
+    def gather_block(idx, line, table, dst):
+        def some(at, first, count):
+            for c in range(count // 16):
+                got = [table[idx[at, c * 16 + r]] for r in range(16)]
+                dst[pl.ds(pl.multiple_of((first + c * 16) * sub, 16 * sub), 16 * sub), :] = jnp.concatenate(got, axis=0).astype(jnp.bfloat16)
+
+        def body(i, carry):
+            some(line + i, i * LANES, LANES)
             return carry
-        lax.fori_loop(0, rows // 16, body, 0)
+
+        lax.fori_loop(0, lines, body, 0)
+        if rest:
+            some(line + lines, lines * LANES, rest)
 
     def widen(src, dst, first):
         def body(c, carry):
@@ -301,37 +311,46 @@
             src_ref=src.at[g, peer], dst_ref=dst.at[g, me], send_sem=s_sem.at[g, k], recv_sem=r_sem.at[g, k],
             device_id={"expert": peer}, device_id_type=MESH)
 
-    def send_blocks(g, idx, stride, table, src, dst, s_sem, r_sem):
-        late = None
-        for k in list(range(1, groups)) + [0]:
-            peer = lax.rem(me + k, groups)
-            gather_block(idx, (g * groups + peer) * stride, table, src.at[g, peer])
-            if late is not None:
-                late.start()
-            late = copy_to(src, dst, g, k, s_sem, r_sem) if k else None
+    def send_blocks(g, idx, table, src, dst, s_sem, r_sem):
+        def body(i, carry):
+            peer = lax.rem(me + i + 1, groups)
+            gather_block(idx, (g * groups + peer) * (lines + (rest > 0)), table, src.at[g, peer])
+
+            @pl.when(i >= 1)
+            def _():
+                copy_to(src, dst, g, i, s_sem, r_sem).start()
+
+            return carry
+
+        lax.fori_loop(0, groups, body, 0)
 
     def take_blocks(g, src, dst, own, first, s_sem, r_sem):
-        for k in range(groups):
+        widen(own.at[g, me], dst, first + me * span)
+
+        def body(k, carry):
             peer = lax.rem(me - k + groups, groups)
-            if k:
-                pltpu.make_async_remote_copy(
-                    src_ref=own.at[g, peer], dst_ref=src.at[g, peer], send_sem=s_sem.at[g, k], recv_sem=r_sem.at[g, k],
-                    device_id={"expert": peer}, device_id_type=MESH).wait_recv()
-                widen(src.at[g, peer], dst, first + peer * span)
-            else:
-                widen(own.at[g, peer], dst, first + peer * span)
+            pltpu.make_async_remote_copy(
+                src_ref=own.at[g, peer], dst_ref=src.at[g, peer], send_sem=s_sem.at[g, k], recv_sem=r_sem.at[g, k],
+                device_id={"expert": peer}, device_id_type=MESH).wait_recv()
+            widen(src.at[g, peer], dst, first + peer * span)
+            return carry
+
+        lax.fori_loop(1, groups, body, 0)
 
     for g in range(GROUPS):
-        send_blocks(g, pack_idx, rows, xr_rows, send, recv, ssem, rsem)
+        send_blocks(g, pack_idx, xr_rows, send, recv, ssem, rsem)
 
     every[me] = count[...]
+    for j in range(2):
+        for b in range(tokens // LANES):
+            gates_v[j * (tokens // LANES) + b:j * (tokens // LANES) + b + 1, :] = gates_ref[j:j + 1, b * LANES:(b + 1) * LANES]
     for k in range(1, groups):
         source = lax.rem(me - k + groups, groups)
         pltpu.make_async_remote_copy(
             src_ref=count, dst_ref=every.at[source], send_sem=csend.at[k], recv_sem=crecv.at[k],
             device_id={"expert": source}, device_id_type=MESH).wait_recv()
     group_tables(me, groups, rows, group_experts, capacity, every, hot, same, rank_ref, pos_ref, lhs_v, ret_v, comb_v, load_ref)
-    tables = [pltpu.make_async_copy(a, b, tsem.at[i + 1]) for i, (a, b) in enumerate(((lhs_v, lhs_idx), (ret_v, ret_idx), (comb_v, comb_idx)))]
+    tables = [pltpu.make_async_copy(a, b, tsem.at[i + 1]) for i, (a, b) in enumerate(((lhs_v, lhs_idx), (ret_v, ret_idx), (comb_v, comb_idx), (gates_v, gates)))]
     for t in tables:
         t.start()
     for t in tables:
@@ -342,7 +361,7 @@
 
         def gather_lhs(e, stage):
             for q in range(capacity):
-                stage[pl.ds(q * sub, sub), :] = rf_rows[lhs_idx[q, e]]
+                stage[pl.ds(q * sub, sub), :] = rf_rows[lhs_idx[e, q]]
 
         def ffn(e, stage):
             slot = lax.rem(e, BUFS)
@@ -368,23 +387,26 @@
             return carry
 
         lax.fori_loop(0, group_experts // 2, body, 0)
-        send_blocks(g, ret_idx, -(-rows // LANES) * LANES, of_rows, rsend, rrecv, rssem, rrsem)
+        send_blocks(g, ret_idx, of_rows, rsend, rrecv, rssem, rrsem)
 
     for g in range(GROUPS):
         take_blocks(g, rrecv, retf, rsend, g * groups * span, rssem, rrsem)
 
-    def combine(c, carry):
-        got = []
-        line, col = c // (LANES // 16), c % (LANES // 16) * 16
-        for r in range(16):
-            row = xr_rows[c * 16 + r]
-            for j in range(2):
-                row = row + gates[j * (tokens // LANES) + line, col + r] * retf_rows[comb_idx[j * (tokens // LANES) + line, col + r]]
-            got.append(row)
-        xr[pl.ds(pl.multiple_of(c * 16 * sub, 16 * sub), 16 * sub), :] = jnp.concatenate(got, axis=0)
+    half = tokens // LANES
+
+    def combine(line, carry):
+        for c in range(LANES // 16):
+            got = []
+            for r in range(16):
+                col = c * 16 + r
+                row = xr_rows[line * LANES + col]
+                for j in range(2):
+                    row = row + gates[j * half + line, col] * retf_rows[comb_idx[j * half + line, col]]
+                got.append(row)
+            xr[pl.ds(pl.multiple_of((line * LANES + c * 16) * sub, 16 * sub), 16 * sub), :] = jnp.concatenate(got, axis=0)
         return carry
 
-    lax.fori_loop(0, tokens // 16, combine, 0)
+    lax.fori_loop(0, half, combine, 0)
     for k in range(sub):
         out_ref[:, k * LANES:(k + 1) * LANES] = xr[pl.ds(k, tokens, stride=sub), :].astype(jnp.bfloat16)
     for g in range(GROUPS):
@@ -402,21 +424,20 @@
     group_experts = local_experts // GROUPS
     sub = model_dim // LANES
     span = rows * sub
-    smem = pl.BlockSpec(memory_space=pltpu.SMEM)
     vmem = pl.BlockSpec(memory_space=pltpu.VMEM)
     hbm = pl.BlockSpec(memory_space=pl.ANY)
     wire = pltpu.VMEM((GROUPS, groups, span, LANES), jnp.bfloat16)
     sems = pltpu.SemaphoreType.DMA((GROUPS, groups))
     table_rows = (
-        -(-(GROUPS * groups * rows) // (8 * LANES)) * 8,
-        capacity,
+        GROUPS * groups * -(-rows // LANES),
+        local_experts,
         GROUPS * groups * -(-rows // LANES),
         2 * tokens // LANES,
     )
     return pl.pallas_call(
         functools.partial(exchange_kernel, groups, rows, capacity),
         out_shape=(jax.ShapeDtypeStruct((tokens, model_dim), jnp.bfloat16), jax.ShapeDtypeStruct((8, LANES), jnp.float32)),
-        in_specs=[smem, vmem, vmem, hbm, hbm],
+        in_specs=[vmem, vmem, vmem, hbm, hbm],
         out_specs=(vmem, vmem),
         scratch_shapes=[
             pltpu.VMEM((2, experts, tokens), jnp.bfloat16),
@@ -426,7 +447,9 @@
             pltpu.VMEM((8, tokens), jnp.float32),
             pltpu.VMEM((8, tokens), jnp.float32),
             *[pltpu.VMEM((r, LANES), jnp.int32) for r in table_rows],
+            pltpu.VMEM((2 * tokens // LANES, LANES), jnp.float32),
             *[pltpu.SMEM((r, LANES), jnp.int32) for r in table_rows],
+            pltpu.SMEM((2 * tokens // LANES, LANES), jnp.float32),
             pltpu.VMEM((tokens, sub, LANES), jnp.float32),
             wire,
             wire,
@@ -443,7 +466,7 @@
             sems, sems, sems, sems,
             pltpu.SemaphoreType.DMA((groups,)),
             pltpu.SemaphoreType.DMA((groups,)),
-            pltpu.SemaphoreType.DMA((4,)),
+            pltpu.SemaphoreType.DMA((5,)),
         ],
         compiler_params=pltpu.CompilerParams(collective_id=0, has_side_effects=True, vmem_limit_bytes=67043328),
         name="expert_exchange",
@@ -460,14 +483,9 @@
         local_experts = w_in.shape[0]
         capacity = tokens * top_k // local_experts
         rows = block_rows(tokens, top_k, groups)
-        gates = gate_weights.T.reshape(-1, LANES)
-        fast, load = compact_step(groups, rows, capacity, gates, expert_ids.T, token_rows, w_in, w_out)
+        fast, load = compact_step(groups, rows, capacity, gate_weights.T, expert_ids.T, token_rows, w_in, w_out)
         overflow = load[0, 0] > rows
-        return lax.cond(
-            overflow,
-            lambda f: padded_step(groups, token_rows, expert_ids, gate_weights, w_in, w_out),
-            lambda f: f,
-            fast,
-        )
+        general = lambda state: (jnp.array(False), padded_step(groups, token_rows, expert_ids, gate_weights, w_in, w_out))
+        return lax.while_loop(lambda state: state[0], general, (overflow, fast))[1]
 
     return jax.shard_map(device_step, mesh=mesh, in_specs=(row_spec, row_spec, row_spec, weight_spec, weight_spec), out_specs=row_spec, check_vma=False)

time: 142 us -> 133 us (0.937)
  Pallas kernels: 134 us -> 127 us
    pallas_call x1, Pallas kernels: 134 us -> 127 us  [compact_step(): pl.pallas_call(functools.partial(exchange_kernel, groups, rows, capacity)...]
where the time goes in v3:
time: 133 us; the launch traced here: 132 us
  Pallas kernels  127 us (95%)
  local copies, waits for them, and re-layouts  4.24 us (3%)
    pallas_call x1, Pallas kernels, compact_step(): pl.pallas_call(functools.partial(exchange_kernel, groups, rows, capacity)...  127 us
    unnamed x1, local copies, waits for them, and re-layouts  3.05 us

profile of v3, /device:TPU:1, one launch (start us, length us, event | category | flops | bytes accessed | tf_op | source)
XLA Modules:
  0.0 132.3 jit_solution(965355174256857571)
XLA Ops:
  0.0 127.2 %expert_exchange.1 = (bf16[2048,512]{1,0:T(8,128)(2,1)}, f32[8,128]{1,0:T(8,128)}) custom-call(f32[2,2048]{1,0:T(2,128)} %bitcast.104, s32[2,2048]{1,0:T(2,128)} %bitcast.95, bf16[2048,512]{1,0:T(8,128)(2,1)} %x_ref.1, bf16[64,512,1024]{2,1,0:T(8,128)(2,1)} %win_ref.1, bf16[64,1024,512]{2,1,0:T(8,128)(2,1)} %wout_ref.1), custom_call_target="tpu_custom_call" | custom-call | tf_op jit(solution)/shard_map/expert_exchange/pallas_call | solution.py:437
  127.2 1.2 slice.12
  129.1 0.2 while.21
  129.3 3.0 %copy.47 = bf16[2048,512]{1,0:T(8,128)(2,1)} copy(bf16[2048,512]{1,0:T(8,128)(2,1)} %get-tuple-element.139) | data formatting | bytes 4194304

commit v4 on v3

--- a/solution.py
+++ b/solution.py
@@ -236,12 +236,12 @@
 
 def exchange_kernel(
     groups, rows, capacity,
-    gates_ref, ids_ref, x_ref, win_ref, wout_ref, out_ref, load_ref,
-    hot, same, count, every, rank_ref, pos_ref, pack_v, lhs_v, ret_v, comb_v, gates_v, pack_idx, lhs_idx, ret_idx, comb_idx, gates,
+    gates_ref, ids_ref, x_hbm, win_ref, wout_ref, out_hbm, load_ref,
+    hot, same, count, every, rank_ref, pos_ref, pack_v, lhs_v, ret_v, comb_v, pack_idx, lhs_idx, ret_idx, comb_idx, wide_gates, x_ref,
     xr_rows, send, recv, rf_rows, stage0, stage1, of_rows, rsend, rrecv, retf_rows, wi, wo,
-    wsem, ssem, rsem, rssem, rrsem, csend, crecv, tsem,
+    wsem, ssem, rsem, rssem, rrsem, csend, crecv, tsem, osem,
 ):
-    tokens, model_dim = x_ref.shape
+    tokens, model_dim = x_hbm.shape
     sub = model_dim // LANES
     local_experts = win_ref.shape[0]
     group_experts = local_experts // GROUPS
@@ -255,19 +255,22 @@
         b = pltpu.make_async_copy(wout_ref.at[e], wo.at[slot], wsem.at[slot, 1])
         return a, b
 
+    x_copy = pltpu.make_async_copy(x_hbm, x_ref, tsem.at[4])
+    x_copy.start()
     for e in range(BUFS):
         for c in fetch(e, e):
             c.start()
     barrier = pltpu.get_barrier_semaphore()
     for k in range(1, groups):
         pl.semaphore_signal(barrier, inc=1, device_id={"expert": lax.rem(me + k, groups)}, device_id_type=MESH)
-    for k in range(sub):
-        xr[pl.ds(k, tokens, stride=sub), :] = x_ref[:, k * LANES:(k + 1) * LANES].astype(jnp.float32)
     retf[pl.ds(GROUPS * groups * span, 8 * sub), :] = jnp.zeros((8 * sub, LANES), jnp.float32)
     experts = hot.shape[1]
     i_e, i_f = iota((experts, experts), 0), iota((experts, experts), 1)
     same[...] = as_bf16((i_e // group_experts == i_f // group_experts) & (i_e < i_f))
     base, counts = local_positions(groups, rows, group_experts, ids_ref, hot, same, count, rank_ref, pos_ref, pack_v)
+    x_copy.wait()
+    for k in range(sub):
+        xr[pl.ds(k, tokens, stride=sub), :] = x_ref[:, k * LANES:(k + 1) * LANES].astype(jnp.float32)
     place_pairs(groups, rows, group_experts, base, counts, ids_ref, hot, same, rank_ref, pos_ref, pack_v)
     pack_copy = pltpu.make_async_copy(pack_v, pack_idx, tsem.at[0])
     pack_copy.start()
@@ -343,14 +346,15 @@
     every[me] = count[...]
     for j in range(2):
         for b in range(tokens // LANES):
-            gates_v[j * (tokens // LANES) + b:j * (tokens // LANES) + b + 1, :] = gates_ref[j:j + 1, b * LANES:(b + 1) * LANES]
+            part = slice(b * LANES, (b + 1) * LANES)
+            wide_gates[j, part, :] = jnp.broadcast_to(gates_ref[j:j + 1, part], (LANES, LANES)).T
     for k in range(1, groups):
         source = lax.rem(me - k + groups, groups)
         pltpu.make_async_remote_copy(
             src_ref=count, dst_ref=every.at[source], send_sem=csend.at[k], recv_sem=crecv.at[k],
             device_id={"expert": source}, device_id_type=MESH).wait_recv()
     group_tables(me, groups, rows, group_experts, capacity, every, hot, same, rank_ref, pos_ref, lhs_v, ret_v, comb_v, load_ref)
-    tables = [pltpu.make_async_copy(a, b, tsem.at[i + 1]) for i, (a, b) in enumerate(((lhs_v, lhs_idx), (ret_v, ret_idx), (comb_v, comb_idx), (gates_v, gates)))]
+    tables = [pltpu.make_async_copy(a, b, tsem.at[i + 1]) for i, (a, b) in enumerate(((lhs_v, lhs_idx), (ret_v, ret_idx), (comb_v, comb_idx)))]
     for t in tables:
         t.start()
     for t in tables:
@@ -401,14 +405,27 @@
                 col = c * 16 + r
                 row = xr_rows[line * LANES + col]
                 for j in range(2):
-                    row = row + gates[j * half + line, col] * retf_rows[comb_idx[j * half + line, col]]
+                    row = row + wide_gates[j, pl.ds(pl.multiple_of(line * LANES, LANES) + col, 1), :] * retf_rows[comb_idx[j * half + line, col]]
                 got.append(row)
             xr[pl.ds(pl.multiple_of((line * LANES + c * 16) * sub, 16 * sub), 16 * sub), :] = jnp.concatenate(got, axis=0)
+        part = pl.ds(pl.multiple_of(line * LANES, LANES), LANES)
+        for k in range(sub):
+            x_ref[part, k * LANES:(k + 1) * LANES] = xr[pl.ds(line * LANES * sub + k, LANES, stride=sub), :].astype(jnp.bfloat16)
+
+        @pl.when(line >= 1)
+        def _():
+            put(line - 1).start()
+
         return carry
 
+    def put(line):
+        part = pl.ds(pl.multiple_of(line * LANES, LANES), LANES)
+        return pltpu.make_async_copy(x_ref.at[part], out_hbm.at[part], osem.at[line])
+
     lax.fori_loop(0, half, combine, 0)
-    for k in range(sub):
-        out_ref[:, k * LANES:(k + 1) * LANES] = xr[pl.ds(k, tokens, stride=sub), :].astype(jnp.bfloat16)
+    put(half - 1).start()
+    for line in range(half):
+        put(line).wait()
     for g in range(GROUPS):
         for k in range(1, groups):
             if g == 0:
@@ -436,9 +453,9 @@
     )
     return pl.pallas_call(
         functools.partial(exchange_kernel, groups, rows, capacity),
-        out_shape=(jax.ShapeDtypeStruct((tokens, model_dim), jnp.bfloat16), jax.ShapeDtypeStruct((8, LANES), jnp.float32)),
-        in_specs=[vmem, vmem, vmem, hbm, hbm],
-        out_specs=(vmem, vmem),
+        out_shape=(jax.ShapeDtypeStruct((tokens, model_dim), jnp.bfloat16), jax.ShapeDtypeStruct((1, 1), jnp.float32)),
+        in_specs=[vmem, vmem, hbm, hbm, hbm],
+        out_specs=(hbm, vmem),
         scratch_shapes=[
             pltpu.VMEM((2, experts, tokens), jnp.bfloat16),
             pltpu.VMEM((experts, experts), jnp.bfloat16),
@@ -447,9 +464,9 @@
             pltpu.VMEM((8, tokens), jnp.float32),
             pltpu.VMEM((8, tokens), jnp.float32),
             *[pltpu.VMEM((r, LANES), jnp.int32) for r in table_rows],
-            pltpu.VMEM((2 * tokens // LANES, LANES), jnp.float32),
             *[pltpu.SMEM((r, LANES), jnp.int32) for r in table_rows],
-            pltpu.SMEM((2 * tokens // LANES, LANES), jnp.float32),
+            pltpu.VMEM((2, tokens, LANES), jnp.float32),
+            pltpu.VMEM((tokens, model_dim), jnp.bfloat16),
             pltpu.VMEM((tokens, sub, LANES), jnp.float32),
             wire,
             wire,
@@ -467,10 +484,19 @@
             pltpu.SemaphoreType.DMA((groups,)),
             pltpu.SemaphoreType.DMA((groups,)),
             pltpu.SemaphoreType.DMA((5,)),
+            pltpu.SemaphoreType.DMA((tokens // LANES,)),
         ],
         compiler_params=pltpu.CompilerParams(collective_id=0, has_side_effects=True, vmem_limit_bytes=67043328),
         name="expert_exchange",
     )(gates, ids, token_rows, w_in, w_out)
+
+
+def hand_over(rows):
+    def kernel(a_ref, o_ref):
+        o_ref[...] = a_ref[...]
+
+    block = pl.BlockSpec((rows.shape[0] // 4, rows.shape[1]), lambda i: (i, 0))
+    return pl.pallas_call(kernel, grid=(4,), in_specs=[block], out_specs=block, out_shape=jax.ShapeDtypeStruct(rows.shape, rows.dtype), name="hand_over")(rows)
 
 
 def solution(mesh):
@@ -484,6 +510,7 @@
         capacity = tokens * top_k // local_experts
         rows = block_rows(tokens, top_k, groups)
         fast, load = compact_step(groups, rows, capacity, gate_weights.T, expert_ids.T, token_rows, w_in, w_out)
+        fast = hand_over(fast)
         overflow = load[0, 0] > rows
         general = lambda state: (jnp.array(False), padded_step(groups, token_rows, expert_ids, gate_weights, w_in, w_out))
         return lax.while_loop(lambda state: state[0], general, (overflow, fast))[1]

time: 133 us -> 131 us (0.985)
  local copies, waits for them, and re-layouts: 4.24 us -> 0.01 us
  Pallas kernels: 127 us -> 129 us
    pallas_call x0 -> x1, Pallas kernels: none -> 3.78 us  [hand_over(): pl.pallas_call(kernel, grid=(4,), in_specs=[block], out_specs=block, out_...]
    unnamed x1 -> x4, local copies, waits for them, and re-layouts: 3.05 us -> 0.01 us
    pallas_call x1, Pallas kernels: 127 us -> 126 us  [compact_step(): pl.pallas_call(functools.partial(exchange_kernel, groups, rows, capacity)...]
where the time goes in v4:
time: 131 us
  Pallas kernels  129 us (98%)
    pallas_call x1, Pallas kernels, compact_step(): pl.pallas_call(functools.partial(exchange_kernel, groups, rows, capacity)...  126 us
    pallas_call x1, Pallas kernels, hand_over(): pl.pallas_call(kernel, grid=(4,), in_specs=[block], out_specs=block, out_...  3.78 us

profile of v4, /device:TPU:1, one launch (start us, length us, event | category | flops | bytes accessed | tf_op | source)
XLA Modules:
  0.0 130.6 jit_solution(5478435418083324406)
XLA Ops:
  0.0 125.7 %expert_exchange.1 = (bf16[2048,512]{1,0:T(8,128)(2,1)}, f32[1,1]{1,0:T(1,128)}) custom-call(f32[2,2048]{1,0:T(2,128)} %bitcast.104, s32[2,2048]{1,0:T(2,128)} %bitcast.95, bf16[2048,512]{1,0:T(8,128)(2,1)} %x_hbm.1, bf16[64,512,1024]{2,1,0:T(8,128)(2,1)} %win_ref.1, bf16[64,1024,512]{2,1,0:T(8,128)(2,1)} %wout_ref.1), custom_call_target="tpu_custom_call" | custom-call | tf_op jit(solution)/shard_map/expert_exchange/pallas_call | solution.py:454
  125.7 0.0 copy-start.2
  125.7 0.0 copy-start.3
  125.7 3.8 %hand_over.1 = bf16[2048,512]{1,0:T(8,128)(2,1)} custom-call(bf16[2048,512]{1,0:T(8,128)(2,1)} %get-tuple-element.138.a_ref), custom_call_target="tpu_custom_call" | custom-call | tf_op jit(solution)/shard_map/hand_over/pallas_call | solution.py:499
  130.2 0.0 copy-done.2
  130.2 0.0 copy-done.3
  130.2 0.2 while.21
Async XLA Ops:
  125.7 4.4 %copy-start.2 = (s32[2048,2]{0,1:T(2,128)S(1)}, s32[2048,2]{0,1:T(2,128)}, u32[]{:S(2)}) copy-start(s32[2048,2]{0,1:T(2,128)} %param.12) | copy-start | bytes 49156
  125.7 4.4 %copy-start.3 = (f32[2048,2]{0,1:T(2,128)S(1)}, f32[2048,2]{0,1:T(2,128)}, u32[]{:S(2)}) copy-start(f32[2048,2]{0,1:T(2,128)} %param.13) | copy-start | bytes 49156

commit v5 on v4

--- a/solution.py
+++ b/solution.py
@@ -92,34 +92,48 @@
     return jnp.concatenate(rows, axis=0)
 
 
-def local_positions(groups, rows, group_experts, ids_ref, hot, same, count_ref, rank_ref, pos_ref, pack_ref):
+def select_row(rows, high_row):
+    total = jnp.zeros_like(rows[0])
+    for i, row in enumerate(rows):
+        total = total + jnp.where(high_row == i, row, 0.0)
+    return total
+
+
+def split_lanes(row):
+    return [row[:, i * LANES:(i + 1) * LANES] for i in range(row.shape[1] // LANES)]
+
+
+def local_counts(experts, ids_ref, hot, count_ref):
     tokens = ids_ref.shape[1]
-    experts = hot.shape[1]
     blocks = tokens // LANES
-    local_experts = experts // groups
+    highs = experts // LANES
 
     def fill(b, carry):
         at = pl.ds(pl.multiple_of(b * LANES, LANES), LANES)
         for j in range(2):
-            hot[j, :, at] = as_bf16(iota((experts, LANES), 0) == ids_ref[j:j + 1, at])
+            hot[j, :, at] = as_bf16(iota((LANES, LANES), 0) == ids_ref[j:j + 1, at] % LANES)
         return carry
 
     lax.fori_loop(0, blocks, fill, 0)
-    part = as_bf16(iota((blocks, tokens), 0) == iota((blocks, tokens), 1) // LANES)
-    below = as_bf16(iota((blocks, blocks), 0) > iota((blocks, blocks), 1))
+    n = highs * blocks
+    row, col = iota((n, n), 0), iota((n, n), 1)
+    below = as_bf16((row // blocks == col // blocks) & (row > col))
+    in_block = iota((n, tokens), 0) % blocks == iota((n, tokens), 1) // LANES
     base, count = [], []
     for j in range(2):
+        part = as_bf16(in_block & (iota((n, tokens), 0) // blocks == ids_ref[j:j + 1, :] // LANES))
         per_block = dot_nt(part, hot[j])
         base.append(dot_f32(below, per_block.astype(jnp.bfloat16)))
-        count.append(jnp.sum(per_block, axis=0, keepdims=True))
+        count.append(jnp.concatenate([jnp.sum(per_block[i * blocks:(i + 1) * blocks], axis=0, keepdims=True) for i in range(highs)], axis=1))
     count_ref[...] = pad_rows(count, 8)
     return base, count
 
 
 def place_pairs(groups, rows, group_experts, base, count, ids_ref, hot, same, rank_ref, pos_ref, pack_ref):
     tokens = ids_ref.shape[1]
-    experts = hot.shape[1]
+    experts = same.shape[0]
     blocks = tokens // LANES
+    highs = experts // LANES
     local_experts = experts // groups
     both = pad_rows([count[0] + count[1]], 8)
     start = dot_f32(both.astype(jnp.bfloat16), same[...])[0:1]
@@ -130,18 +144,23 @@
     earlier = iota((LANES, LANES), 0) < iota((LANES, LANES), 1)
     found = None
     table_rows = pack_ref.shape[0]
+    n = highs * blocks
     for j in range(2):
         at = first if j == 0 else first + count[0]
-        high = jnp.floor(at * (1.0 / 64.0))
-        look = dot_f32(pad_rows([base[j], high, at - 64.0 * high], 32).astype(jnp.bfloat16), hot[j])
+        coarse = jnp.floor(at * (1.0 / 64.0))
+        lhs = [base[j]] + split_lanes(coarse) + split_lanes(at - 64.0 * coarse)
+        look = dot_f32(pad_rows(lhs, -(-(n + 2 * highs) // 16) * 16).astype(jnp.bfloat16), hot[j])
         for b in range(blocks):
             cols = slice(b * LANES, (b + 1) * LANES)
             row = ids_ref[j:j + 1, cols]
+            high_row = row // LANES
             wide = jnp.broadcast_to(row.astype(jnp.float32), (LANES, LANES))
             same_id = (wide.T == wide) & earlier
-            rank = jnp.sum(jnp.where(same_id, 1.0, 0.0), axis=0, keepdims=True) + look[b:b + 1, cols]
+            rank = jnp.sum(jnp.where(same_id, 1.0, 0.0), axis=0, keepdims=True)
+            rank = rank + select_row([look[i * blocks + b:i * blocks + b + 1, cols] for i in range(highs)], high_row)
+            offset = select_row([64.0 * look[n + i:n + i + 1, cols] + look[n + highs + i:n + highs + i + 1, cols] for i in range(highs)], high_row)
             rank_ref[j:j + 1, cols] = rank
-            pos_ref[j:j + 1, cols] = rank + 64.0 * look[blocks:blocks + 1, cols] + look[blocks + 1:blocks + 2, cols]
+            pos_ref[j:j + 1, cols] = rank + offset
         pos = pos_ref[j:j + 1, :]
         pos_ref[j:j + 1, :] = pos - (stride - rows) * jnp.floor((pos + 0.5) * (1.0 / stride))
         pos = pos.astype(jnp.int32)
@@ -155,8 +174,8 @@
     pack_ref[...] = jnp.clip(found.astype(jnp.int32), 0, tokens - 1)
 
 
-def group_tables(me, groups, rows, group_experts, capacity, every, hot, same, rank_ref, pos_ref, lhs_ref, ret_ref, comb_ref, load_ref):
-    experts = hot.shape[1]
+def group_tables(me, groups, rows, group_experts, capacity, every, ids_ref, hot, same, rank_ref, pos_ref, lhs_ref, ret_ref, comb_ref, load_ref):
+    experts = same.shape[0]
     tokens = hot.shape[2]
     local_experts = experts // groups
     blocks = tokens // LANES
@@ -226,11 +245,12 @@
         own = jnp.zeros((1, experts), jnp.float32)
         for s in range(groups):
             own = own + jnp.where(me == s, kept[j][s], 0.0)
-        bound = dot_f32(pad_rows([own], 16).astype(jnp.bfloat16), hot[j])
+        bound = dot_f32(pad_rows(split_lanes(own), 16).astype(jnp.bfloat16), hot[j])
+        bound = select_row([bound[i:i + 1] for i in range(experts // LANES)], ids_ref[j:j + 1, :] // LANES)
         none = float(GROUPS * groups * rows)
         for b in range(blocks):
             cols = slice(b * LANES, (b + 1) * LANES)
-            take = jnp.where(rank_ref[j:j + 1, cols] < bound[0:1, cols], pos_ref[j:j + 1, cols], none)
+            take = jnp.where(rank_ref[j:j + 1, cols] < bound[:, cols], pos_ref[j:j + 1, cols], none)
             comb_ref[j * blocks + b:j * blocks + b + 1, :] = jnp.clip(take.astype(jnp.int32), 0, GROUPS * groups * rows)
 
 
@@ -264,10 +284,10 @@
     for k in range(1, groups):
         pl.semaphore_signal(barrier, inc=1, device_id={"expert": lax.rem(me + k, groups)}, device_id_type=MESH)
     retf[pl.ds(GROUPS * groups * span, 8 * sub), :] = jnp.zeros((8 * sub, LANES), jnp.float32)
-    experts = hot.shape[1]
+    experts = same.shape[0]
     i_e, i_f = iota((experts, experts), 0), iota((experts, experts), 1)
     same[...] = as_bf16((i_e // group_experts == i_f // group_experts) & (i_e < i_f))
-    base, counts = local_positions(groups, rows, group_experts, ids_ref, hot, same, count, rank_ref, pos_ref, pack_v)
+    base, counts = local_counts(experts, ids_ref, hot, count)
     x_copy.wait()
     for k in range(sub):
         xr[pl.ds(k, tokens, stride=sub), :] = x_ref[:, k * LANES:(k + 1) * LANES].astype(jnp.float32)
@@ -353,7 +373,7 @@
         pltpu.make_async_remote_copy(
             src_ref=count, dst_ref=every.at[source], send_sem=csend.at[k], recv_sem=crecv.at[k],
             device_id={"expert": source}, device_id_type=MESH).wait_recv()
-    group_tables(me, groups, rows, group_experts, capacity, every, hot, same, rank_ref, pos_ref, lhs_v, ret_v, comb_v, load_ref)
+    group_tables(me, groups, rows, group_experts, capacity, every, ids_ref, hot, same, rank_ref, pos_ref, lhs_v, ret_v, comb_v, load_ref)
     tables = [pltpu.make_async_copy(a, b, tsem.at[i + 1]) for i, (a, b) in enumerate(((lhs_v, lhs_idx), (ret_v, ret_idx), (comb_v, comb_idx)))]
     for t in tables:
         t.start()
@@ -457,7 +477,7 @@
         in_specs=[vmem, vmem, hbm, hbm, hbm],
         out_specs=(hbm, vmem),
         scratch_shapes=[
-            pltpu.VMEM((2, experts, tokens), jnp.bfloat16),
+            pltpu.VMEM((2, LANES, tokens), jnp.bfloat16),
             pltpu.VMEM((experts, experts), jnp.bfloat16),
             pltpu.VMEM((8, experts), jnp.float32),
             pltpu.VMEM((groups, 8, experts), jnp.float32),
@@ -492,11 +512,29 @@
 
 
 def hand_over(rows):
-    def kernel(a_ref, o_ref):
-        o_ref[...] = a_ref[...]
-
-    block = pl.BlockSpec((rows.shape[0] // 4, rows.shape[1]), lambda i: (i, 0))
-    return pl.pallas_call(kernel, grid=(4,), in_specs=[block], out_specs=block, out_shape=jax.ShapeDtypeStruct(rows.shape, rows.dtype), name="hand_over")(rows)
+    parts = 8
+    size = rows.shape[0] // parts
+
+    def kernel(a_ref, o_ref, buf, sem_in, sem_out):
+        part = [pl.ds(i * size, size) for i in range(parts)]
+        take = [pltpu.make_async_copy(a_ref.at[p], buf.at[p], sem_in.at[i]) for i, p in enumerate(part)]
+        give = [pltpu.make_async_copy(buf.at[p], o_ref.at[p], sem_out.at[i]) for i, p in enumerate(part)]
+        for t in take:
+            t.start()
+        for t, g in zip(take, give):
+            t.wait()
+            g.start()
+        for g in give:
+            g.wait()
+
+    return pl.pallas_call(
+        kernel,
+        in_specs=[pl.BlockSpec(memory_space=pl.ANY)],
+        out_specs=pl.BlockSpec(memory_space=pl.ANY),
+        out_shape=jax.ShapeDtypeStruct(rows.shape, rows.dtype),
+        scratch_shapes=[pltpu.VMEM(rows.shape, rows.dtype), pltpu.SemaphoreType.DMA((parts,)), pltpu.SemaphoreType.DMA((parts,))],
+        name="hand_over",
+    )(rows)
 
 
 def solution(mesh):

time: 131 us -> 129 us (0.985)
    pallas_call x1, Pallas kernels: 3.78 us -> 2.4 us  [hand_over(): pl.pallas_call(kernel, in_specs=[pl.BlockSpec(memory_space=pl.ANY)], out_...]
where the time goes in v5:
time: 129 us
  Pallas kernels  128 us (99%)
    pallas_call x1, Pallas kernels, compact_step(): pl.pallas_call(functools.partial(exchange_kernel, groups, rows, capacity)...  126 us

profile of v5, /device:TPU:1, one launch (start us, length us, event | category | flops | bytes accessed | tf_op | source)
XLA Modules:
  0.0 129.1 jit_solution(13687603748294090476)
XLA Ops:
  0.0 125.6 %expert_exchange.1 = (bf16[2048,512]{1,0:T(8,128)(2,1)}, f32[1,1]{1,0:T(1,128)}) custom-call(f32[2,2048]{1,0:T(2,128)} %bitcast.104, s32[2,2048]{1,0:T(2,128)} %bitcast.95, bf16[2048,512]{1,0:T(8,128)(2,1)} %x_hbm.1, bf16[64,512,1024]{2,1,0:T(8,128)(2,1)} %win_ref.1, bf16[64,1024,512]{2,1,0:T(8,128)(2,1)} %wout_ref.1), custom_call_target="tpu_custom_call" | custom-call | tf_op jit(solution)/shard_map/expert_exchange/pallas_call | solution.py:474
  125.6 0.0 copy-start.2
  125.6 0.0 copy-start.3
  125.6 2.4 %hand_over.1 = bf16[2048,512]{1,0:T(8,128)(2,1)} custom-call(bf16[2048,512]{1,0:T(8,128)(2,1)} %get-tuple-element.138.a_ref), custom_call_target="tpu_custom_call" | custom-call | tf_op jit(solution)/shard_map/hand_over/pallas_call | solution.py:530
  128.6 0.0 copy-done.2
  128.7 0.0 copy-done.3
  128.7 0.2 while.21
Async XLA Ops:
  125.6 3.1 %copy-start.2 = (s32[2048,2]{0,1:T(2,128)S(1)}, s32[2048,2]{0,1:T(2,128)}, u32[]{:S(2)}) copy-start(s32[2048,2]{0,1:T(2,128)} %param.12) | copy-start | bytes 49156
  125.6 3.1 %copy-start.3 = (f32[2048,2]{0,1:T(2,128)S(1)}, f32[2048,2]{0,1:T(2,128)}, u32[]{:S(2)}) copy-start(f32[2048,2]{0,1:T(2,128)} %param.13) | copy-start | bytes 49156

commit v6 on v5

--- a/solution.py
+++ b/solution.py
@@ -8,7 +8,7 @@
 from jax.sharding import PartitionSpec as P
 
 GROUPS = 2
-BUFS = 3
+BUFS = 5
 LANES = 128
 MESH = pl.DeviceIdType.MESH
 
@@ -69,6 +69,10 @@
     return (mean * 19 // 16 + 15) // 16 * 16
 
 
+def total_rows(tokens, top_k, groups):
+    return (tokens * top_k // groups * 9 // 8 + 15) // 16 * 16
+
+
 def dot_f32(a, b):
     return jnp.dot(a, b, preferred_element_type=jnp.float32)
 
@@ -129,7 +133,7 @@
     return base, count
 
 
-def place_pairs(groups, rows, group_experts, base, count, ids_ref, hot, same, rank_ref, pos_ref, pack_ref):
+def place_pairs(groups, rows, out_rows, group_experts, base, count, ids_ref, hot, same, rank_ref, pos_ref, pack_ref):
     tokens = ids_ref.shape[1]
     experts = same.shape[0]
     blocks = tokens // LANES
@@ -139,17 +143,20 @@
     start = dot_f32(both.astype(jnp.bfloat16), same[...])[0:1]
     lane = iota((1, experts), 1)
     block_of = (lane % local_experts // group_experts) * groups + lane // local_experts
-    stride = -(-rows // LANES) * LANES
-    first = (block_of * stride).astype(jnp.float32) + start
+    stride = -(-out_rows // LANES) * LANES
+    back_first = (block_of * rows).astype(jnp.float32) + start[:, :experts]
+    out_first = (lane // local_experts * stride).astype(jnp.float32) + start[:, experts:]
     earlier = iota((LANES, LANES), 0) < iota((LANES, LANES), 1)
     found = None
     table_rows = pack_ref.shape[0]
     n = highs * blocks
     for j in range(2):
-        at = first if j == 0 else first + count[0]
-        coarse = jnp.floor(at * (1.0 / 64.0))
-        lhs = [base[j]] + split_lanes(coarse) + split_lanes(at - 64.0 * coarse)
-        look = dot_f32(pad_rows(lhs, -(-(n + 2 * highs) // 16) * 16).astype(jnp.bfloat16), hot[j])
+        lhs = [base[j]]
+        for first in (out_first, back_first):
+            at = first if j == 0 else first + count[0]
+            coarse = jnp.floor(at * (1.0 / 64.0))
+            lhs += split_lanes(coarse) + split_lanes(at - 64.0 * coarse)
+        look = dot_f32(pad_rows(lhs, -(-(n + 4 * highs) // 16) * 16).astype(jnp.bfloat16), hot[j])
         for b in range(blocks):
             cols = slice(b * LANES, (b + 1) * LANES)
             row = ids_ref[j:j + 1, cols]
@@ -158,12 +165,13 @@
             same_id = (wide.T == wide) & earlier
             rank = jnp.sum(jnp.where(same_id, 1.0, 0.0), axis=0, keepdims=True)
             rank = rank + select_row([look[i * blocks + b:i * blocks + b + 1, cols] for i in range(highs)], high_row)
-            offset = select_row([64.0 * look[n + i:n + i + 1, cols] + look[n + highs + i:n + highs + i + 1, cols] for i in range(highs)], high_row)
+            offsets = []
+            for m in (n, n + 2 * highs):
+                offsets.append(select_row([64.0 * look[m + i:m + i + 1, cols] + look[m + highs + i:m + highs + i + 1, cols] for i in range(highs)], high_row))
             rank_ref[j:j + 1, cols] = rank
-            pos_ref[j:j + 1, cols] = rank + offset
-        pos = pos_ref[j:j + 1, :]
-        pos_ref[j:j + 1, :] = pos - (stride - rows) * jnp.floor((pos + 0.5) * (1.0 / stride))
-        pos = pos.astype(jnp.int32)
+            pos_ref[j + 2:j + 3, cols] = rank + offsets[0]
+            pos_ref[j:j + 1, cols] = rank + offsets[1]
+        pos = pos_ref[j + 2:j + 3, :].astype(jnp.int32)
         token = iota((LANES, tokens), 1)
         high_t = as_bf16(iota((table_rows, tokens), 0) == pos // LANES)
         low = iota((LANES, tokens), 0) == pos % LANES
@@ -174,15 +182,17 @@
     pack_ref[...] = jnp.clip(found.astype(jnp.int32), 0, tokens - 1)
 
 
-def group_tables(me, groups, rows, group_experts, capacity, every, ids_ref, hot, same, rank_ref, pos_ref, lhs_ref, ret_ref, comb_ref, load_ref):
+def group_tables(me, groups, rows, out_rows, group_experts, capacity, every, ids_ref, hot, same, rank_ref, pos_ref, lhs_ref, ret_ref, comb_ref, load_ref):
     experts = same.shape[0]
     tokens = hot.shape[2]
     local_experts = experts // groups
     blocks = tokens // LANES
     c = [[every[s, j:j + 1, :] for s in range(groups)] for j in range(2)]
     both = pad_rows([c[0][s] + c[1][s] for s in range(groups)], 8)
-    start = dot_f32(both.astype(jnp.bfloat16), same[...])
-    load_ref[...] = jnp.broadcast_to(jnp.max(start + both), load_ref.shape)
+    starts = dot_f32(both.astype(jnp.bfloat16), same[...])
+    start, out_start = starts[:, :experts], starts[:, experts:]
+    over = jnp.maximum(jnp.max(start + both) - rows, jnp.max(out_start + both) - out_rows)
+    load_ref[...] = jnp.broadcast_to(over, load_ref.shape)
     kept = [[None] * groups, [None] * groups]
     used = jnp.zeros((1, experts), jnp.float32)
     for j in range(2):
@@ -198,7 +208,7 @@
         ret_v = []
         for j in range(2):
             edge = start[s:s + 1] if j == 0 else start[s:s + 1] + c[0][s]
-            v = s * rows + edge - slot
+            v = s * out_rows + edge + out_start[s:s + 1] - start[s:s + 1] - slot
             slots.append(slot)
             steps.append(v - last)
             last = v
@@ -224,7 +234,7 @@
     for i in range(2 * groups):
         at = 4 * groups + i
         lhs = lhs + jnp.where(q >= tall[:local_experts, at:at + 1], tall[:local_experts, at + 2 * groups:at + 2 * groups + 1], 0.0)
-    lhs_ref[...] = jnp.clip(lhs.astype(jnp.int32), 0, groups * rows - 1)
+    lhs_ref[...] = jnp.clip(lhs.astype(jnp.int32), 0, groups * out_rows - 1)
 
     width = -(-rows // LANES) * LANES
     p = iota((1, width), 1).astype(jnp.float32)
@@ -255,7 +265,7 @@
 
 
 def exchange_kernel(
-    groups, rows, capacity,
+    groups, rows, out_rows, capacity,
     gates_ref, ids_ref, x_hbm, win_ref, wout_ref, out_hbm, load_ref,
     hot, same, count, every, rank_ref, pos_ref, pack_v, lhs_v, ret_v, comb_v, pack_idx, lhs_idx, ret_idx, comb_idx, wide_gates, x_ref,
     xr_rows, send, recv, rf_rows, stage0, stage1, of_rows, rsend, rrecv, retf_rows, wi, wo,
@@ -286,12 +296,13 @@
     retf[pl.ds(GROUPS * groups * span, 8 * sub), :] = jnp.zeros((8 * sub, LANES), jnp.float32)
     experts = same.shape[0]
     i_e, i_f = iota((experts, experts), 0), iota((experts, experts), 1)
-    same[...] = as_bf16((i_e // group_experts == i_f // group_experts) & (i_e < i_f))
+    same[:, :experts] = as_bf16((i_e // group_experts == i_f // group_experts) & (i_e < i_f))
+    same[:, experts:] = as_bf16((i_e // local_experts == i_f // local_experts) & (i_e < i_f))
     base, counts = local_counts(experts, ids_ref, hot, count)
     x_copy.wait()
     for k in range(sub):
         xr[pl.ds(k, tokens, stride=sub), :] = x_ref[:, k * LANES:(k + 1) * LANES].astype(jnp.float32)
-    place_pairs(groups, rows, group_experts, base, counts, ids_ref, hot, same, rank_ref, pos_ref, pack_v)
+    place_pairs(groups, rows, out_rows, group_experts, base, counts, ids_ref, hot, same, rank_ref, pos_ref, pack_v)
     pack_copy = pltpu.make_async_copy(pack_v, pack_idx, tsem.at[0])
     pack_copy.start()
     pl.semaphore_wait(barrier, groups - 1)
@@ -305,63 +316,76 @@
         count_copy(k).start()
     pack_copy.wait()
 
-    lines, rest = divmod(rows, LANES)
-
-    def gather_block(idx, line, table, dst):
-        def some(at, first, count):
-            for c in range(count // 16):
-                got = [table[idx[at, c * 16 + r]] for r in range(16)]
+    def gather_rows(idx, line, low, high, table, dst):
+        def some(at, col, first, size):
+            for c in range(size // 16):
+                got = [table[idx[at, col + c * 16 + r]] for r in range(16)]
                 dst[pl.ds(pl.multiple_of((first + c * 16) * sub, 16 * sub), 16 * sub), :] = jnp.concatenate(got, axis=0).astype(jnp.bfloat16)
 
+        head = -low % LANES
+        if head:
+            some(line + low // LANES, low % LANES, 0, head)
+        lines, rest = divmod(high - low - head, LANES)
+        first = (low + head) // LANES
+
         def body(i, carry):
-            some(line + i, i * LANES, LANES)
+            some(line + first + i, 0, head + i * LANES, LANES)
             return carry
 
         lax.fori_loop(0, lines, body, 0)
         if rest:
-            some(line + lines, lines * LANES, rest)
+            some(line + first + lines, 0, head + lines * LANES, rest)
 
     def widen(src, dst, first):
         def body(c, carry):
             part = pl.multiple_of(c * 16 * sub, 16 * sub)
             dst[pl.ds(pl.multiple_of(first + part, 16), 16 * sub), :] = src[pl.ds(part, 16 * sub), :].astype(jnp.float32)
             return carry
-        lax.fori_loop(0, rows // 16, body, 0)
-
-    def copy_to(src, dst, g, k, s_sem, r_sem):
+        lax.fori_loop(0, src.shape[0] // (16 * sub), body, 0)
+
+    def out_part(ref, g, peer):
+        low, high = ((0, rows), (rows, out_rows))[g]
+        return ref.at[peer, pl.ds(low * sub, (high - low) * sub)]
+
+    def back_part(ref, g, peer):
+        return ref.at[g, peer]
+
+    def copy_to(part, src, dst, g, k, s_sem, r_sem):
         peer = lax.rem(me + k, groups)
         return pltpu.make_async_remote_copy(
-            src_ref=src.at[g, peer], dst_ref=dst.at[g, me], send_sem=s_sem.at[g, k], recv_sem=r_sem.at[g, k],
+            src_ref=part(src, g, peer), dst_ref=part(dst, g, me), send_sem=s_sem.at[g, k], recv_sem=r_sem.at[g, k],
             device_id={"expert": peer}, device_id_type=MESH)
 
-    def send_blocks(g, idx, table, src, dst, s_sem, r_sem):
+    def send_blocks(g, part, gather, src, dst, s_sem, r_sem):
         def body(i, carry):
             peer = lax.rem(me + i + 1, groups)
-            gather_block(idx, (g * groups + peer) * (lines + (rest > 0)), table, src.at[g, peer])
+            gather(peer, part(src, g, peer))
 
             @pl.when(i >= 1)
             def _():
-                copy_to(src, dst, g, i, s_sem, r_sem).start()
+                copy_to(part, src, dst, g, i, s_sem, r_sem).start()
 
             return carry
 
         lax.fori_loop(0, groups, body, 0)
 
-    def take_blocks(g, src, dst, own, first, s_sem, r_sem):
-        widen(own.at[g, me], dst, first + me * span)
+    def take_blocks(g, part, src, dst, own, first, s_sem, r_sem):
+        widen(part(own, g, me), dst, first(me))
 
         def body(k, carry):
             peer = lax.rem(me - k + groups, groups)
             pltpu.make_async_remote_copy(
-                src_ref=own.at[g, peer], dst_ref=src.at[g, peer], send_sem=s_sem.at[g, k], recv_sem=r_sem.at[g, k],
+                src_ref=part(own, g, peer), dst_ref=part(src, g, peer), send_sem=s_sem.at[g, k], recv_sem=r_sem.at[g, k],
                 device_id={"expert": peer}, device_id_type=MESH).wait_recv()
-            widen(src.at[g, peer], dst, first + peer * span)
+            widen(part(src, g, peer), dst, first(peer))
             return carry
 
         lax.fori_loop(1, groups, body, 0)
 
+    out_lines, back_lines = -(-out_rows // LANES), -(-rows // LANES)
     for g in range(GROUPS):
-        send_blocks(g, pack_idx, xr_rows, send, recv, ssem, rsem)
+        low, high = ((0, rows), (rows, out_rows))[g]
+        send_blocks(g, out_part, lambda peer, dst: gather_rows(pack_idx, peer * out_lines, low, high, xr_rows, dst), send, recv, ssem, rsem)
 
     every[me] = count[...]
     for j in range(2):
@@ -373,7 +397,7 @@
         pltpu.make_async_remote_copy(
             src_ref=count, dst_ref=every.at[source], send_sem=csend.at[k], recv_sem=crecv.at[k],
             device_id={"expert": source}, device_id_type=MESH).wait_recv()
-    group_tables(me, groups, rows, group_experts, capacity, every, ids_ref, hot, same, rank_ref, pos_ref, lhs_v, ret_v, comb_v, load_ref)
+    group_tables(me, groups, rows, out_rows, group_experts, capacity, every, ids_ref, hot, same, rank_ref, pos_ref, lhs_v, ret_v, comb_v, load_ref)
     tables = [pltpu.make_async_copy(a, b, tsem.at[i + 1]) for i, (a, b) in enumerate(((lhs_v, lhs_idx), (ret_v, ret_idx), (comb_v, comb_idx)))]
     for t in tables:
         t.start()
@@ -381,7 +405,7 @@
         t.wait()
 
     for g in range(GROUPS):
-        take_blocks(g, recv, rf, send, 0, ssem, rsem)
+        take_blocks(g, out_part, recv, rf, send, lambda peer: (peer * out_rows + g * rows) * sub, ssem, rsem)
 
         def gather_lhs(e, stage):
             for q in range(capacity):
@@ -411,10 +435,10 @@
             return carry
 
         lax.fori_loop(0, group_experts // 2, body, 0)
-        send_blocks(g, ret_idx, of_rows, rsend, rrecv, rssem, rrsem)
+        send_blocks(g, back_part, lambda peer, dst: gather_rows(ret_idx, (g * groups + peer) * back_lines, 0, rows, of_rows, dst), rsend, rrecv, rssem, rrsem)
 
     for g in range(GROUPS):
-        take_blocks(g, rrecv, retf, rsend, g * groups * span, rssem, rrsem)
+        take_blocks(g, back_part, rrecv, retf, rsend, lambda peer: (g * groups + peer) * span, rssem, rrsem)
 
     half = tokens // LANES
 
@@ -450,11 +474,11 @@
         for k in range(1, groups):
             if g == 0:
                 count_copy(k).wait_send()
-            copy_to(send, recv, g, k, ssem, rsem).wait_send()
-            copy_to(rsend, rrecv, g, k, rssem, rrsem).wait_send()
-
-
-def compact_step(groups, rows, capacity, gates, ids, token_rows, w_in, w_out):
+            copy_to(out_part, send, recv, g, k, ssem, rsem).wait_send()
+            copy_to(back_part, rsend, rrecv, g, k, rssem, rrsem).wait_send()
+
+
+def compact_step(groups, rows, out_rows, capacity, gates, ids, token_rows, w_in, w_out):
     tokens, model_dim = token_rows.shape
     local_experts, _, hidden_dim = w_in.shape
     experts = local_experts * groups
@@ -466,19 +490,19 @@
     wire = pltpu.VMEM((GROUPS, groups, span, LANES), jnp.bfloat16)
     sems = pltpu.SemaphoreType.DMA((GROUPS, groups))
     table_rows = (
-        GROUPS * groups * -(-rows // LANES),
+        groups * -(-out_rows // LANES),
         local_experts,
         GROUPS * groups * -(-rows // LANES),
         2 * tokens // LANES,
     )
     return pl.pallas_call(
-        functools.partial(exchange_kernel, groups, rows, capacity),
+        functools.partial(exchange_kernel, groups, rows, out_rows, capacity),
         out_shape=(jax.ShapeDtypeStruct((tokens, model_dim), jnp.bfloat16), jax.ShapeDtypeStruct((1, 1), jnp.float32)),
         in_specs=[vmem, vmem, hbm, hbm, hbm],
         out_specs=(hbm, vmem),
         scratch_shapes=[
             pltpu.VMEM((2, LANES, tokens), jnp.bfloat16),
-            pltpu.VMEM((experts, experts), jnp.bfloat16),
+            pltpu.VMEM((experts, 2 * experts), jnp.bfloat16),
             pltpu.VMEM((8, experts), jnp.float32),
             pltpu.VMEM((groups, 8, experts), jnp.float32),
             pltpu.VMEM((8, tokens), jnp.float32),
@@ -488,9 +512,9 @@
             pltpu.VMEM((2, tokens, LANES), jnp.float32),
             pltpu.VMEM((tokens, model_dim), jnp.bfloat16),
             pltpu.VMEM((tokens, sub, LANES), jnp.float32),
-            wire,
-            wire,
-            pltpu.VMEM((groups * rows, sub, LANES), jnp.float32),
+            pltpu.VMEM((groups, out_rows * sub, LANES), jnp.bfloat16),
+            pltpu.VMEM((groups, out_rows * sub, LANES), jnp.bfloat16),
+            pltpu.VMEM((groups * out_rows, sub, LANES), jnp.float32),
             pltpu.VMEM((capacity * sub, LANES), jnp.float32),
             pltpu.VMEM((capacity * sub, LANES), jnp.float32),
             pltpu.VMEM((group_experts * capacity, sub, LANES), jnp.float32),
@@ -547,9 +571,9 @@
         local_experts = w_in.shape[0]
         capacity = tokens * top_k // local_experts
         rows = block_rows(tokens, top_k, groups)
-        fast, load = compact_step(groups, rows, capacity, gate_weights.T, expert_ids.T, token_rows, w_in, w_out)
+        fast, load = compact_step(groups, rows, total_rows(tokens, top_k, groups), capacity, gate_weights.T, expert_ids.T, token_rows, w_in, w_out)
         fast = hand_over(fast)
-        overflow = load[0, 0] > rows
+        overflow = load[0, 0] > 0.0
         general = lambda state: (jnp.array(False), padded_step(groups, token_rows, expert_ids, gate_weights, w_in, w_out))
         return lax.while_loop(lambda state: state[0], general, (overflow, fast))[1]
 

time: 129 us -> 128 us (level)
  Pallas kernels: 128 us -> 126 us
    pallas_call x1, Pallas kernels: 126 us -> 124 us  [compact_step(): pl.pallas_call(functools.partial(exchange_kernel, groups, rows, out_rows,...]
where the time goes in v6:
time: 128 us
  Pallas kernels  126 us (98%)
    pallas_call x1, Pallas kernels, compact_step(): pl.pallas_call(functools.partial(exchange_kernel, groups, rows, out_rows,...  124 us

profile of v6, /device:TPU:1, one launch (start us, length us, event | category | flops | bytes accessed | tf_op | source)
XLA Modules:
  0.0 127.6 jit_solution(6497590286136051751)
XLA Ops:
  0.0 124.1 %expert_exchange.1 = (bf16[2048,512]{1,0:T(8,128)(2,1)}, f32[1,1]{1,0:T(1,128)}) custom-call(f32[2,2048]{1,0:T(2,128)} %bitcast.104, s32[2,2048]{1,0:T(2,128)} %bitcast.95, bf16[2048,512]{1,0:T(8,128)(2,1)} %x_hbm.1, bf16[64,512,1024]{2,1,0:T(8,128)(2,1)} %win_ref.1, bf16[64,1024,512]{2,1,0:T(8,128)(2,1)} %wout_ref.1), custom_call_target="tpu_custom_call" | custom-call | tf_op jit(solution)/shard_map/expert_exchange/pallas_call | solution.py:498
  124.1 0.0 copy-start.2
  124.1 0.0 copy-start.3
  124.1 2.4 %hand_over.1 = bf16[2048,512]{1,0:T(8,128)(2,1)} custom-call(bf16[2048,512]{1,0:T(8,128)(2,1)} %get-tuple-element.138.a_ref), custom_call_target="tpu_custom_call" | custom-call | tf_op jit(solution)/shard_map/hand_over/pallas_call | solution.py:554
  127.1 0.0 copy-done.2
  127.1 0.0 copy-done.3
  127.2 0.2 while.21
Async XLA Ops:
  124.1 3.1 %copy-start.2 = (s32[2048,2]{0,1:T(2,128)S(1)}, s32[2048,2]{0,1:T(2,128)}, u32[]{:S(2)}) copy-start(s32[2048,2]{0,1:T(2,128)} %param.12) | copy-start | bytes 49156
  124.1 3.1 %copy-start.3 = (f32[2048,2]{0,1:T(2,128)S(1)}, f32[2048,2]{0,1:T(2,128)}, u32[]{:S(2)}) copy-start(f32[2048,2]{0,1:T(2,128)} %param.13) | copy-start | bytes 49156

commit v7 on v6

--- a/solution.py
+++ b/solution.py
@@ -277,6 +277,7 @@
     group_experts = local_experts // GROUPS
     me = lax.axis_index("expert")
     span = rows * sub
+    bits = [2 ** b for b in range(groups.bit_length() - 1)]
     stages = (stage0, stage1)
     xr, rf, of, retf = (r.reshape(r.shape[0] * sub, LANES) for r in (xr_rows, rf_rows, of_rows, retf_rows))
 
@@ -350,20 +351,27 @@
     def back_part(ref, g, peer):
         return ref.at[g, peer]
 
-    def copy_to(part, src, dst, g, k, s_sem, r_sem):
-        peer = lax.rem(me + k, groups)
+    def turn(i):
+        k = groups - 1 - 2 * (i % (groups // 2)) - i // (groups // 2)
+        peer = 0
+        for size in bits:
+            peer = peer + size * ((me // size + k // size) % 2)
+        return k, peer
+
+    def copy_to(part, src, dst, g, i, s_sem, r_sem):
+        k, peer = turn(i)
         return pltpu.make_async_remote_copy(
             src_ref=part(src, g, peer), dst_ref=part(dst, g, me), send_sem=s_sem.at[g, k], recv_sem=r_sem.at[g, k],
             device_id={"expert": peer}, device_id_type=MESH)
 
     def send_blocks(g, part, gather, src, dst, s_sem, r_sem):
         def body(i, carry):
-            peer = lax.rem(me + i + 1, groups)
+            peer = turn(i)[1]
             gather(peer, part(src, g, peer))
 
             @pl.when(i >= 1)
             def _():
-                copy_to(part, src, dst, g, i, s_sem, r_sem).start()
+                copy_to(part, src, dst, g, i - 1, s_sem, r_sem).start()
 
             return carry
 
@@ -372,15 +380,15 @@
     def take_blocks(g, part, src, dst, own, first, s_sem, r_sem):
         widen(part(own, g, me), dst, first(me))
 
-        def body(k, carry):
-            peer = lax.rem(me - k + groups, groups)
+        def body(i, carry):
+            k, peer = turn(i)
             pltpu.make_async_remote_copy(
                 src_ref=part(own, g, peer), dst_ref=part(src, g, peer), send_sem=s_sem.at[g, k], recv_sem=r_sem.at[g, k],
                 device_id={"expert": peer}, device_id_type=MESH).wait_recv()
             widen(part(src, g, peer), dst, first(peer))
             return carry
 
-        lax.fori_loop(1, groups, body, 0)
+        lax.fori_loop(0, groups - 1, body, 0)
 
     out_lines, back_lines = -(-out_rows // LANES), -(-rows // LANES)
     for g in range(GROUPS):
@@ -471,11 +479,11 @@
     for line in range(half):
         put(line).wait()
     for g in range(GROUPS):
-        for k in range(1, groups):
+        for i in range(groups - 1):
             if g == 0:
-                count_copy(k).wait_send()
-            copy_to(out_part, send, recv, g, k, ssem, rsem).wait_send()
-            copy_to(back_part, rsend, rrecv, g, k, rssem, rrsem).wait_send()
+                count_copy(i + 1).wait_send()
+            copy_to(out_part, send, recv, g, i, ssem, rsem).wait_send()
+            copy_to(back_part, rsend, rrecv, g, i, rssem, rrsem).wait_send()
 
 
 def compact_step(groups, rows, out_rows, capacity, gates, ids, token_rows, w_in, w_out):

time: 128 us -> 129 us (level); the launches traced: 128 us -> 127 us
  no operation moved by 1% of the time
where the time goes in v7:
time: 129 us; the launch traced here: 127 us
  Pallas kernels  126 us (98%)
    pallas_call x1, Pallas kernels, compact_step(): pl.pallas_call(functools.partial(exchange_kernel, groups, rows, out_rows,...  124 us

profile of v7, /device:TPU:1, one launch (start us, length us, event | category | flops | bytes accessed | tf_op | source)
XLA Modules:
  0.0 127.2 jit_solution(11776910710107961080)
XLA Ops:
  0.0 123.7 %expert_exchange.1 = (bf16[2048,512]{1,0:T(8,128)(2,1)}, f32[1,1]{1,0:T(1,128)}) custom-call(f32[2,2048]{1,0:T(2,128)} %bitcast.104, s32[2,2048]{1,0:T(2,128)} %bitcast.95, bf16[2048,512]{1,0:T(8,128)(2,1)} %x_hbm.1, bf16[64,512,1024]{2,1,0:T(8,128)(2,1)} %win_ref.1, bf16[64,1024,512]{2,1,0:T(8,128)(2,1)} %wout_ref.1), custom_call_target="tpu_custom_call" | custom-call | tf_op jit(solution)/shard_map/expert_exchange/pallas_call | solution.py:506
  123.7 0.0 copy-start.2
  123.7 0.0 copy-start.3
  123.7 2.4 %hand_over.1 = bf16[2048,512]{1,0:T(8,128)(2,1)} custom-call(bf16[2048,512]{1,0:T(8,128)(2,1)} %get-tuple-element.138.a_ref), custom_call_target="tpu_custom_call" | custom-call | tf_op jit(solution)/shard_map/hand_over/pallas_call | solution.py:562
  126.8 0.0 copy-done.2
  126.8 0.0 copy-done.3
  126.8 0.2 while.21
Async XLA Ops:
  123.7 3.1 %copy-start.2 = (s32[2048,2]{0,1:T(2,128)S(1)}, s32[2048,2]{0,1:T(2,128)}, u32[]{:S(2)}) copy-start(s32[2048,2]{0,1:T(2,128)} %param.12) | copy-start | bytes 49156
  123.7 3.1 %copy-start.3 = (f32[2048,2]{0,1:T(2,128)S(1)}, f32[2048,2]{0,1:T(2,128)}, u32[]{:S(2)}) copy-start(f32[2048,2]{0,1:T(2,128)} %param.13) | copy-start | bytes 49156

commit v8 on v6

--- a/solution.py
+++ b/solution.py
@@ -8,7 +8,7 @@
 from jax.sharding import PartitionSpec as P
 
 GROUPS = 2
-BUFS = 5
+BUFS = 4
 LANES = 128
 MESH = pl.DeviceIdType.MESH
 
@@ -73,6 +73,12 @@
     return (tokens * top_k // groups * 9 // 8 + 15) // 16 * 16
 
 
+def stages_of(tokens, top_k, groups, local_experts):
+    mean = tokens * top_k // groups
+    cuts = [0, mean * 13 // 32 // 16 * 16, mean * 20 // 32 // 16 * 16, total_rows(tokens, top_k, groups)]
+    return [(cuts[i], cuts[i + 1], local_experts * (2 + i) // 4) for i in range(3)]
+
+
 def dot_f32(a, b):
     return jnp.dot(a, b, preferred_element_type=jnp.float32)
 
@@ -142,21 +148,17 @@
     both = pad_rows([count[0] + count[1]], 8)
     start = dot_f32(both.astype(jnp.bfloat16), same[...])[0:1]
     lane = iota((1, experts), 1)
-    block_of = (lane % local_experts // group_experts) * groups + lane // local_experts
     stride = -(-out_rows // LANES) * LANES
-    back_first = (block_of * rows).astype(jnp.float32) + start[:, :experts]
-    out_first = (lane // local_experts * stride).astype(jnp.float32) + start[:, experts:]
+    first = (lane // local_experts * stride).astype(jnp.float32) + start
     earlier = iota((LANES, LANES), 0) < iota((LANES, LANES), 1)
     found = None
     table_rows = pack_ref.shape[0]
     n = highs * blocks
     for j in range(2):
-        lhs = [base[j]]
-        for first in (out_first, back_first):
-            at = first if j == 0 else first + count[0]
-            coarse = jnp.floor(at * (1.0 / 64.0))
-            lhs += split_lanes(coarse) + split_lanes(at - 64.0 * coarse)
-        look = dot_f32(pad_rows(lhs, -(-(n + 4 * highs) // 16) * 16).astype(jnp.bfloat16), hot[j])
+        at = first if j == 0 else first + count[0]
+        coarse = jnp.floor(at * (1.0 / 64.0))
+        lhs = [base[j]] + split_lanes(coarse) + split_lanes(at - 64.0 * coarse)
+        look = dot_f32(pad_rows(lhs, -(-(n + 2 * highs) // 16) * 16).astype(jnp.bfloat16), hot[j])
         for b in range(blocks):
             cols = slice(b * LANES, (b + 1) * LANES)
             row = ids_ref[j:j + 1, cols]
@@ -165,13 +167,12 @@
             same_id = (wide.T == wide) & earlier
             rank = jnp.sum(jnp.where(same_id, 1.0, 0.0), axis=0, keepdims=True)
             rank = rank + select_row([look[i * blocks + b:i * blocks + b + 1, cols] for i in range(highs)], high_row)
-            offsets = []
-            for m in (n, n + 2 * highs):
-                offsets.append(select_row([64.0 * look[m + i:m + i + 1, cols] + look[m + highs + i:m + highs + i + 1, cols] for i in range(highs)], high_row))
+            offset = select_row([64.0 * look[n + i:n + i + 1, cols] + look[n + highs + i:n + highs + i + 1, cols] for i in range(highs)], high_row)
             rank_ref[j:j + 1, cols] = rank
-            pos_ref[j + 2:j + 3, cols] = rank + offsets[0]
-            pos_ref[j:j + 1, cols] = rank + offsets[1]
-        pos = pos_ref[j + 2:j + 3, :].astype(jnp.int32)
+            pos_ref[j:j + 1, cols] = rank + offset
+        pos = pos_ref[j:j + 1, :]
+        pos_ref[j:j + 1, :] = pos - (stride - out_rows) * jnp.floor((pos + 0.5) * (1.0 / stride))
+        pos = pos.astype(jnp.int32)
         token = iota((LANES, tokens), 1)
         high_t = as_bf16(iota((table_rows, tokens), 0) == pos // LANES)
         low = iota((LANES, tokens), 0) == pos % LANES
@@ -182,17 +183,19 @@
     pack_ref[...] = jnp.clip(found.astype(jnp.int32), 0, tokens - 1)
 
 
-def group_tables(me, groups, rows, out_rows, group_experts, capacity, every, ids_ref, hot, same, rank_ref, pos_ref, lhs_ref, ret_ref, comb_ref, load_ref):
+def group_tables(me, groups, rows, out_rows, back, group_experts, capacity, every, ids_ref, hot, same, rank_ref, pos_ref, lhs_ref, ret_ref, comb_ref, load_ref):
     experts = same.shape[0]
     tokens = hot.shape[2]
     local_experts = experts // groups
     blocks = tokens // LANES
     c = [[every[s, j:j + 1, :] for s in range(groups)] for j in range(2)]
     both = pad_rows([c[0][s] + c[1][s] for s in range(groups)], 8)
-    starts = dot_f32(both.astype(jnp.bfloat16), same[...])
-    start, out_start = starts[:, :experts], starts[:, experts:]
-    over = jnp.maximum(jnp.max(start + both) - rows, jnp.max(out_start + both) - out_rows)
-    load_ref[...] = jnp.broadcast_to(over, load_ref.shape)
+    start = dot_f32(both.astype(jnp.bfloat16), same[...])
+    local = iota((8, experts), 1) % local_experts
+    over = jnp.maximum(start + both - out_rows, jnp.where(local == group_experts, start - rows, -1.0))
+    for _, high, done in back[:-1]:
+        over = jnp.maximum(over, jnp.where(local == done, high - start, -1.0))
+    load_ref[...] = jnp.broadcast_to(jnp.max(over), load_ref.shape)
     kept = [[None] * groups, [None] * groups]
     used = jnp.zeros((1, experts), jnp.float32)
     for j in range(2):
@@ -200,7 +203,7 @@
             kept[j][s] = jnp.clip(capacity - used, 0.0, c[j][s])
             used = used + c[j][s]
     lane = iota((1, experts), 1)
-    in_group = lane % group_experts
+    local = lane % local_experts
     slot = jnp.zeros((1, experts), jnp.float32)
     slots, steps, edges, jumps = [], [], [], []
     last = jnp.zeros((1, experts), jnp.float32)
@@ -208,15 +211,15 @@
         ret_v = []
         for j in range(2):
             edge = start[s:s + 1] if j == 0 else start[s:s + 1] + c[0][s]
-            v = s * out_rows + edge + out_start[s:s + 1] - start[s:s + 1] - slot
+            v = s * out_rows + edge - slot
             slots.append(slot)
             steps.append(v - last)
             last = v
             edges.append(edge)
-            ret_v.append((in_group * capacity).astype(jnp.float32) + slot - edge)
+            ret_v.append((local * capacity).astype(jnp.float32) + slot - edge)
             slot = slot + kept[j][s]
         before = jnp.concatenate([jnp.zeros((1, 1), jnp.float32), ret_v[1][:, :-1]], axis=1)
-        jumps.append(ret_v[0] - jnp.where(in_group == 0, 0.0, before))
+        jumps.append(ret_v[0] - jnp.where(local == 0, 0.0, before))
         jumps.append(ret_v[1] - ret_v[0])
 
     def mine(parts):
@@ -236,20 +239,19 @@
         lhs = lhs + jnp.where(q >= tall[:local_experts, at:at + 1], tall[:local_experts, at + 2 * groups:at + 2 * groups + 1], 0.0)
     lhs_ref[...] = jnp.clip(lhs.astype(jnp.int32), 0, groups * out_rows - 1)
 
-    width = -(-rows // LANES) * LANES
+    width = -(-out_rows // LANES) * LANES
     p = iota((1, width), 1).astype(jnp.float32)
-    for g in range(GROUPS):
-        part = tall[g * group_experts:(g + 1) * group_experts]
-        for s in range(groups):
-            total = jnp.zeros((group_experts, width), jnp.float32)
-            for j in range(2):
-                i = 2 * s + j
-                total = total + jnp.where(p >= part[:, i:i + 1], part[:, 2 * groups + i:2 * groups + i + 1], 0.0)
-            row = p + jnp.sum(total, axis=0, keepdims=True)
-            row = jnp.clip(row.astype(jnp.int32), 0, group_experts * capacity - 1)
-            for i in range(width // LANES):
-                at = (g * groups + s) * (width // LANES) + i
-                ret_ref[at:at + 1, :] = row[:, i * LANES:(i + 1) * LANES]
+    part = tall[:local_experts]
+    for s in range(groups):
+        total = jnp.zeros((local_experts, width), jnp.float32)
+        for j in range(2):
+            i = 2 * s + j
+            total = total + jnp.where(p >= part[:, i:i + 1], part[:, 2 * groups + i:2 * groups + i + 1], 0.0)
+        row = p + jnp.sum(total, axis=0, keepdims=True)
+        row = jnp.clip(row.astype(jnp.int32), 0, local_experts * capacity - 1)
+        for i in range(width // LANES):
+            at = s * (width // LANES) + i
+            ret_ref[at:at + 1, :] = row[:, i * LANES:(i + 1) * LANES]
 
     for j in range(2):
         own = jnp.zeros((1, experts), jnp.float32)
@@ -257,15 +259,15 @@
             own = own + jnp.where(me == s, kept[j][s], 0.0)
         bound = dot_f32(pad_rows(split_lanes(own), 16).astype(jnp.bfloat16), hot[j])
         bound = select_row([bound[i:i + 1] for i in range(experts // LANES)], ids_ref[j:j + 1, :] // LANES)
-        none = float(GROUPS * groups * rows)
+        none = float(groups * out_rows)
         for b in range(blocks):
             cols = slice(b * LANES, (b + 1) * LANES)
             take = jnp.where(rank_ref[j:j + 1, cols] < bound[:, cols], pos_ref[j:j + 1, cols], none)
-            comb_ref[j * blocks + b:j * blocks + b + 1, :] = jnp.clip(take.astype(jnp.int32), 0, GROUPS * groups * rows)
+            comb_ref[j * blocks + b:j * blocks + b + 1, :] = jnp.clip(take.astype(jnp.int32), 0, groups * out_rows)
 
 
 def exchange_kernel(
-    groups, rows, out_rows, capacity,
+    groups, rows, out_rows, back, capacity,
     gates_ref, ids_ref, x_hbm, win_ref, wout_ref, out_hbm, load_ref,
     hot, same, count, every, rank_ref, pos_ref, pack_v, lhs_v, ret_v, comb_v, pack_idx, lhs_idx, ret_idx, comb_idx, wide_gates, x_ref,
     xr_rows, send, recv, rf_rows, stage0, stage1, of_rows, rsend, rrecv, retf_rows, wi, wo,
@@ -293,11 +295,10 @@
     barrier = pltpu.get_barrier_semaphore()
     for k in range(1, groups):
         pl.semaphore_signal(barrier, inc=1, device_id={"expert": lax.rem(me + k, groups)}, device_id_type=MESH)
-    retf[pl.ds(GROUPS * groups * span, 8 * sub), :] = jnp.zeros((8 * sub, LANES), jnp.float32)
+    retf[pl.ds(groups * out_rows * sub, 8 * sub), :] = jnp.zeros((8 * sub, LANES), jnp.float32)
     experts = same.shape[0]
     i_e, i_f = iota((experts, experts), 0), iota((experts, experts), 1)
-    same[:, :experts] = as_bf16((i_e // group_experts == i_f // group_experts) & (i_e < i_f))
-    same[:, experts:] = as_bf16((i_e // local_experts == i_f // local_experts) & (i_e < i_f))
+    same[...] = as_bf16((i_e // local_experts == i_f // local_experts) & (i_e < i_f))
     base, counts = local_counts(experts, ids_ref, hot, count)
     x_copy.wait()
     for k in range(sub):
@@ -322,7 +323,7 @@
                 got = [table[idx[at, col + c * 16 + r]] for r in range(16)]
                 dst[pl.ds(pl.multiple_of((first + c * 16) * sub, 16 * sub), 16 * sub), :] = jnp.concatenate(got, axis=0).astype(jnp.bfloat16)
 
-        head = -low % LANES
+        head = min(-low % LANES, high - low)
         if head:
             some(line + low // LANES, low % LANES, 0, head)
         lines, rest = divmod(high - low - head, LANES)
@@ -348,7 +349,8 @@
         return ref.at[peer, pl.ds(low * sub, (high - low) * sub)]
 
     def back_part(ref, g, peer):
-        return ref.at[g, peer]
+        low, high, _ = back[g]
+        return ref.at[peer, pl.ds(low * sub, (high - low) * sub)]
 
     def copy_to(part, src, dst, g, k, s_sem, r_sem):
         peer = lax.rem(me + k, groups)
@@ -382,7 +384,7 @@
 
         lax.fori_loop(1, groups, body, 0)
 
-    out_lines, back_lines = -(-out_rows // LANES), -(-rows // LANES)
+    out_lines = -(-out_rows // LANES)
     for g in range(GROUPS):
         low, high = ((0, rows), (rows, out_rows))[g]
         send_blocks(g, out_part, lambda peer, dst: gather_rows(pack_idx, peer * out_lines, low, high, xr_rows, dst), send, recv, ssem, rsem)
@@ -397,34 +399,36 @@
         pltpu.make_async_remote_copy(
             src_ref=count, dst_ref=every.at[source], send_sem=csend.at[k], recv_sem=crecv.at[k],
             device_id={"expert": source}, device_id_type=MESH).wait_recv()
-    group_tables(me, groups, rows, out_rows, group_experts, capacity, every, ids_ref, hot, same, rank_ref, pos_ref, lhs_v, ret_v, comb_v, load_ref)
+    group_tables(me, groups, rows, out_rows, back, group_experts, capacity, every, ids_ref, hot, same, rank_ref, pos_ref, lhs_v, ret_v, comb_v, load_ref)
     tables = [pltpu.make_async_copy(a, b, tsem.at[i + 1]) for i, (a, b) in enumerate(((lhs_v, lhs_idx), (ret_v, ret_idx), (comb_v, comb_idx)))]
     for t in tables:
         t.start()
     for t in tables:
         t.wait()
 
-    for g in range(GROUPS):
-        take_blocks(g, out_part, recv, rf, send, lambda peer: (peer * out_rows + g * rows) * sub, ssem, rsem)
-
-        def gather_lhs(e, stage):
-            for q in range(capacity):
-                stage[pl.ds(q * sub, sub), :] = rf_rows[lhs_idx[e, q]]
-
-        def ffn(e, stage):
-            slot = lax.rem(e, BUFS)
-            for c in fetch(e, slot):
-                c.wait()
-            lhs = jnp.concatenate([stage[pl.ds(k, capacity, stride=sub), :] for k in range(sub)], axis=1).astype(jnp.bfloat16)
-            hidden = jax.nn.gelu(dot_f32(lhs, wi[slot])).astype(jnp.bfloat16)
-            out = dot_f32(hidden, wo[slot]).astype(jnp.bfloat16).astype(jnp.float32)
-            at = (e - g * group_experts) * capacity * sub
-            for k in range(sub):
-                of[pl.ds(at + k, capacity, stride=sub), :] = out[:, k * LANES:(k + 1) * LANES]
+    def gather_lhs(e, stage):
+        for q in range(capacity):
+            stage[pl.ds(q * sub, sub), :] = rf_rows[lhs_idx[e, q]]
+
+    def ffn(e, stage):
+        slot = lax.rem(e, BUFS)
+        for c in fetch(e, slot):
+            c.wait()
+        lhs = jnp.concatenate([stage[pl.ds(k, capacity, stride=sub), :] for k in range(sub)], axis=1).astype(jnp.bfloat16)
+        hidden = jax.nn.gelu(dot_f32(lhs, wi[slot])).astype(jnp.bfloat16)
+        out = dot_f32(hidden, wo[slot]).astype(jnp.bfloat16).astype(jnp.float32)
+        at = e * capacity * sub
+        for k in range(sub):
+            of[pl.ds(at + k, capacity, stride=sub), :] = out[:, k * LANES:(k + 1) * LANES]
+
+    first_expert = 0
+    for b, (low, high, done) in enumerate(back):
+        if b < GROUPS:
+            take_blocks(b, out_part, recv, rf, send, lambda peer: (peer * out_rows + b * rows) * sub, ssem, rsem)
 
         def body(i, carry):
             for half in range(2):
-                e = g * group_experts + i * 2 + half
+                e = first_expert + i * 2 + half
                 gather_lhs(e, stages[half])
                 ffn(e, stages[half])
 
@@ -434,11 +438,12 @@
                         c.start()
             return carry
 
-        lax.fori_loop(0, group_experts // 2, body, 0)
-        send_blocks(g, back_part, lambda peer, dst: gather_rows(ret_idx, (g * groups + peer) * back_lines, 0, rows, of_rows, dst), rsend, rrecv, rssem, rrsem)
-
-    for g in range(GROUPS):
-        take_blocks(g, back_part, rrecv, retf, rsend, lambda peer: (g * groups + peer) * span, rssem, rrsem)
+        lax.fori_loop(0, (done - first_expert) // 2, body, 0)
+        first_expert = done
+        send_blocks(b, back_part, lambda peer, dst: gather_rows(ret_idx, peer * out_lines, low, high, of_rows, dst), rsend, rrecv, rssem, rrsem)
+
+    for b, (low, high, done) in enumerate(back):
+        take_blocks(b, back_part, rrecv, retf, rsend, lambda peer: (peer * out_rows + low) * sub, rssem, rrsem)
 
     half = tokens // LANES
 
@@ -475,7 +480,9 @@
             if g == 0:
                 count_copy(k).wait_send()
             copy_to(out_part, send, recv, g, k, ssem, rsem).wait_send()
-            copy_to(back_part, rsend, rrecv, g, k, rssem, rrsem).wait_send()
+    for b in range(len(back)):
+        for k in range(1, groups):
+            copy_to(back_part, rsend, rrecv, b, k, rssem, rrsem).wait_send()
 
 
 def compact_step(groups, rows, out_rows, capacity, gates, ids, token_rows, w_in, w_out):
@@ -487,22 +494,24 @@
     span = rows * sub
     vmem = pl.BlockSpec(memory_space=pltpu.VMEM)
     hbm = pl.BlockSpec(memory_space=pl.ANY)
-    wire = pltpu.VMEM((GROUPS, groups, span, LANES), jnp.bfloat16)
+    wire = pltpu.VMEM((groups, out_rows * sub, LANES), jnp.bfloat16)
+    back = stages_of(tokens, 2, groups, local_experts)
+    back_sems = pltpu.SemaphoreType.DMA((len(back), groups))
     sems = pltpu.SemaphoreType.DMA((GROUPS, groups))
     table_rows = (
         groups * -(-out_rows // LANES),
         local_experts,
-        GROUPS * groups * -(-rows // LANES),
+        groups * -(-out_rows // LANES),
         2 * tokens // LANES,
     )
     return pl.pallas_call(
-        functools.partial(exchange_kernel, groups, rows, out_rows, capacity),
+        functools.partial(exchange_kernel, groups, rows, out_rows, back, capacity),
         out_shape=(jax.ShapeDtypeStruct((tokens, model_dim), jnp.bfloat16), jax.ShapeDtypeStruct((1, 1), jnp.float32)),
         in_specs=[vmem, vmem, hbm, hbm, hbm],
         out_specs=(hbm, vmem),
         scratch_shapes=[
             pltpu.VMEM((2, LANES, tokens), jnp.bfloat16),
-            pltpu.VMEM((experts, 2 * experts), jnp.bfloat16),
+            pltpu.VMEM((experts, experts), jnp.bfloat16),
             pltpu.VMEM((8, experts), jnp.float32),
             pltpu.VMEM((groups, 8, experts), jnp.float32),
             pltpu.VMEM((8, tokens), jnp.float32),
@@ -512,19 +521,19 @@
             pltpu.VMEM((2, tokens, LANES), jnp.float32),
             pltpu.VMEM((tokens, model_dim), jnp.bfloat16),
             pltpu.VMEM((tokens, sub, LANES), jnp.float32),
-            pltpu.VMEM((groups, out_rows * sub, LANES), jnp.bfloat16),
-            pltpu.VMEM((groups, out_rows * sub, LANES), jnp.bfloat16),
+            wire,
+            wire,
             pltpu.VMEM((groups * out_rows, sub, LANES), jnp.float32),
             pltpu.VMEM((capacity * sub, LANES), jnp.float32),
             pltpu.VMEM((capacity * sub, LANES), jnp.float32),
-            pltpu.VMEM((group_experts * capacity, sub, LANES), jnp.float32),
+            pltpu.VMEM((local_experts * capacity, sub, LANES), jnp.float32),
             wire,
             wire,
-            pltpu.VMEM((GROUPS * groups * rows + 8, sub, LANES), jnp.float32),
+            pltpu.VMEM((groups * out_rows + 8, sub, LANES), jnp.float32),
             pltpu.VMEM((BUFS, model_dim, hidden_dim), jnp.bfloat16),
             pltpu.VMEM((BUFS, hidden_dim, model_dim), jnp.bfloat16),
             pltpu.SemaphoreType.DMA((BUFS, 2)),
-            sems, sems, sems, sems,
+            sems, sems, back_sems, back_sems,
             pltpu.SemaphoreType.DMA((groups,)),
             pltpu.SemaphoreType.DMA((groups,)),
             pltpu.SemaphoreType.DMA((5,)),

time: 128 us -> 124 us (0.969)
  Pallas kernels: 126 us -> 123 us
    pallas_call x1, Pallas kernels: 124 us -> 121 us  [compact_step(): pl.pallas_call(functools.partial(exchange_kernel, groups, rows, out_rows,...]
where the time goes in v8:
time: 124 us
  Pallas kernels  123 us (99%)
    pallas_call x1, Pallas kernels, compact_step(): pl.pallas_call(functools.partial(exchange_kernel, groups, rows, out_rows,...  121 us

profile of v8, /device:TPU:1, one launch (start us, length us, event | category | flops | bytes accessed | tf_op | source)
XLA Modules:
  0.0 124.1 jit_solution(11394809130297346953)
XLA Ops:
  0.0 120.6 %expert_exchange.1 = (bf16[2048,512]{1,0:T(8,128)(2,1)}, f32[1,1]{1,0:T(1,128)}) custom-call(f32[2,2048]{1,0:T(2,128)} %bitcast.104, s32[2,2048]{1,0:T(2,128)} %bitcast.95, bf16[2048,512]{1,0:T(8,128)(2,1)} %x_hbm.1, bf16[64,512,1024]{2,1,0:T(8,128)(2,1)} %win_ref.1, bf16[64,1024,512]{2,1,0:T(8,128)(2,1)} %wout_ref.1), custom_call_target="tpu_custom_call" | custom-call | tf_op jit(solution)/shard_map/expert_exchange/pallas_call | solution.py:507
  120.6 0.0 copy-start.2
  120.6 0.0 copy-start.3
  120.7 2.4 %hand_over.1 = bf16[2048,512]{1,0:T(8,128)(2,1)} custom-call(bf16[2048,512]{1,0:T(8,128)(2,1)} %get-tuple-element.138.a_ref), custom_call_target="tpu_custom_call" | custom-call | tf_op jit(solution)/shard_map/hand_over/pallas_call | solution.py:563
  123.7 0.0 copy-done.2
  123.7 0.0 copy-done.3
  123.7 0.2 while.21
Async XLA Ops:
  120.6 3.1 %copy-start.2 = (s32[2048,2]{0,1:T(2,128)S(1)}, s32[2048,2]{0,1:T(2,128)}, u32[]{:S(2)}) copy-start(s32[2048,2]{0,1:T(2,128)} %param.12) | copy-start | bytes 49156
  120.6 3.1 %copy-start.3 = (f32[2048,2]{0,1:T(2,128)S(1)}, f32[2048,2]{0,1:T(2,128)}, u32[]{:S(2)}) copy-start(f32[2048,2]{0,1:T(2,128)} %param.13) | copy-start | bytes 49156

commit v9 on v8

--- a/solution.py
+++ b/solution.py
@@ -545,7 +545,7 @@
 
 
 def hand_over(rows):
-    parts = 8
+    parts = 16
     size = rows.shape[0] // parts
 
     def kernel(a_ref, o_ref, buf, sem_in, sem_out):

time: 124 us -> 125 us (level)
  no operation moved by 1% of the time
where the time goes in v9:
time: 125 us; the launch traced here: 124 us
  Pallas kernels  123 us (98%)
    pallas_call x1, Pallas kernels, compact_step(): pl.pallas_call(functools.partial(exchange_kernel, groups, rows, out_rows,...  121 us
    pallas_call x1, Pallas kernels, hand_over(): pl.pallas_call(kernel, in_specs=[pl.BlockSpec(memory_space=pl.ANY)], out_...  2.58 us

profile of v9, /device:TPU:1, one launch (start us, length us, event | category | flops | bytes accessed | tf_op | source)
XLA Modules:
  0.0 124.3 jit_solution(13294948330371148511)
XLA Ops:
  0.0 120.6 %expert_exchange.1 = (bf16[2048,512]{1,0:T(8,128)(2,1)}, f32[1,1]{1,0:T(1,128)}) custom-call(f32[2,2048]{1,0:T(2,128)} %bitcast.104, s32[2,2048]{1,0:T(2,128)} %bitcast.95, bf16[2048,512]{1,0:T(8,128)(2,1)} %x_hbm.1, bf16[64,512,1024]{2,1,0:T(8,128)(2,1)} %win_ref.1, bf16[64,1024,512]{2,1,0:T(8,128)(2,1)} %wout_ref.1), custom_call_target="tpu_custom_call" | custom-call | tf_op jit(solution)/shard_map/expert_exchange/pallas_call | solution.py:507
  120.6 0.0 copy-start.2
  120.6 0.0 copy-start.3
  120.7 2.6 %hand_over.1 = bf16[2048,512]{1,0:T(8,128)(2,1)} custom-call(bf16[2048,512]{1,0:T(8,128)(2,1)} %get-tuple-element.138.a_ref), custom_call_target="tpu_custom_call" | custom-call | tf_op jit(solution)/shard_map/hand_over/pallas_call | solution.py:563
  123.9 0.0 copy-done.2
  123.9 0.0 copy-done.3
  123.9 0.2 while.21
Async XLA Ops:
  120.6 3.2 %copy-start.2 = (s32[2048,2]{0,1:T(2,128)S(1)}, s32[2048,2]{0,1:T(2,128)}, u32[]{:S(2)}) copy-start(s32[2048,2]{0,1:T(2,128)} %param.12) | copy-start | bytes 49156
  120.6 3.2 %copy-start.3 = (f32[2048,2]{0,1:T(2,128)S(1)}, f32[2048,2]{0,1:T(2,128)}, u32[]{:S(2)}) copy-start(f32[2048,2]{0,1:T(2,128)} %param.13) | copy-start | bytes 49156
